TPU v7x, 32 devices: a whole 2x2x4 slice. The times are simulated.
32 devices in a mesh: dp: 8 (over z, y), neg: 4 (over x, core).
Axes of the slice: x: 2, y: 2, z: 4, core: 2. Of those that a mesh axis runs over, the one named last changes fastest.
Arguments:
- user_embed: bfloat16 [24576, 256], P(('dp', 'neg')), may hold values from -25 to 25
- positive_embed: bfloat16 [24576, 256], P(('dp', 'neg')), may hold values from -6 to 6
- positive_ids: int32 [24576], P(('dp', 'neg')), may hold values from 0 to 1048575
- token_weights: int32 [24576], P(('dp', 'neg')), may hold values from 1 to 5
- offsets: int32 [8, 25], P('dp'), may hold values from 0 to 3072, as said below
- negative_embed: bfloat16 [32768, 256], P('neg'), may hold values from -6 to 6
- negative_ids: int32 [32768], P('neg'), may hold values from 0 to 1048575
Outputs:
- token_loss: float32 [24576], P(('dp', 'neg'))
- mean_loss: float32 [], replicated
Inputs may be any that keep to these rules, and one draw needn't show every extreme that they name: `offsets`: each row starts at 0 and does not fall; every user holds 2 or more slots; in every draw some group fills all 3072 slots.
All inputs are finite; a program needn't handle non-finite values.
Results may differ from a plain program's by a relative error of at most 0.0003.
Values may be sent and summed in bfloat16 or wider, within the bound.
No kernel may reach another device: no remote copies, remote signals or barrier semaphores. Data moves between devices by JAX's collectives and lax.ppermute only.
A program may use at most 64 MiB of HBM per device.

v0:
```python
import math

import jax
import jax.numpy as jnp
from jax import lax
from jax.sharding import PartitionSpec as P

floor_value = -1e30


def merged(value, axis, join):
    pieces = jax.tree.map(lambda part: lax.all_gather(part, axis), value)
    head = jax.tree.map(lambda part: part[0], pieces)
    tail = jax.tree.map(lambda part: part[1:], pieces)
    total, _ = lax.scan(lambda total, share: (join(total, share), None), head, tail)
    return total


def shard_partials(rows, row_ids, columns, column_ids, scale):
    logits = (
        lax.dot_general(rows, columns, (((1,), (1,)), ((), ())), preferred_element_type=jnp.float32)
        * scale
    )
    hit = row_ids[:, None] == column_ids[None, :]
    peak = jnp.max(jnp.where(hit, floor_value, logits), axis=1)
    summed = jnp.sum(jnp.where(hit, 0.0, jnp.exp(logits - peak[:, None])), axis=1)
    return (peak, summed)


def combine(first, second):
    peak = jnp.maximum(first[0], second[0])
    return (peak, first[1] * jnp.exp(first[0] - peak) + second[1] * jnp.exp(second[0] - peak))


def shards(
    user_embed, positive_embed, positive_ids, token_weights, offsets, negative_embed, negative_ids
):
    tok_rows = user_embed.shape[0]
    width = user_embed.shape[1]
    scale = 3.0 / math.sqrt(width)
    positions = lax.axis_index("neg") * tok_rows + jnp.arange(tok_rows, dtype=jnp.int32)
    ends = offsets[0, 1:]
    last_slot = jnp.any(positions[:, None] + 1 == ends[None, :], axis=1)
    live = (positions < offsets[0, -1]) & jnp.logical_not(last_slot)
    weight = token_weights.astype(jnp.float32)
    live_weight = weight * live.astype(jnp.float32)
    rows = lax.all_gather(user_embed, "neg", axis=0, tiled=True)
    row_ids = lax.all_gather(positive_ids, "neg", axis=0, tiled=True)
    number = rows.shape[0]
    block = math.gcd(number, 512)
    blocks = rows.reshape(number // block, block, width)
    id_blocks = row_ids.reshape(number // block, block)

    def one_block(pair):
        return shard_partials(pair[0], pair[1], negative_embed, negative_ids, scale)

    peaks, sums = lax.map(one_block, (blocks, id_blocks))
    new_peaks = peaks.reshape(number)
    new_sums = sums.reshape(number)
    peaks = new_peaks
    sums = new_sums
    peaks, sums = merged((peaks, sums), "neg", combine)
    own_start = lax.axis_index("neg") * tok_rows
    peaks = lax.dynamic_slice_in_dim(peaks, own_start, tok_rows, 0)
    sums = lax.dynamic_slice_in_dim(sums, own_start, tok_rows, 0)
    positive = (
        jnp.sum(user_embed.astype(jnp.float32) * positive_embed.astype(jnp.float32), axis=1) * scale
    )
    top = jnp.maximum(peaks, positive)
    lse = top + jnp.log(sums * jnp.exp(peaks - top) + jnp.exp(positive - top))
    token_loss = jnp.where(live, lse - positive, 0.0).astype(jnp.float32)
    weighted = jnp.sum(weight * token_loss)
    total, count = lax.psum((weighted, jnp.sum(live_weight)), ("dp", "neg"))
    return (token_loss, total / count)


def solution(mesh):
    in_specs = (
        P(("dp", "neg"), None),
        P(("dp", "neg"), None),
        P(("dp", "neg")),
        P(("dp", "neg")),
        P("dp", None),
        P("neg", None),
        P("neg"),
    )
    out_specs = (P(("dp", "neg")), P())
    return jax.shard_map(shards, mesh=mesh, in_specs=in_specs, out_specs=out_specs, check_vma=False)
```

profile of v0, /device:TPU:0, one launch (start us, length us, event | category | flops | bytes accessed | tf_op | source)
XLA Modules:
  0.0 153.4 jit_solution(13548246562837746475)
XLA Ops:
  7.2 0.0 all-gather.5.cloned.1.call-start
  7.2 0.7 all-gather.5.cloned.1.call-update
  7.9 0.7 reshape.22
  8.6 6.2 %all-gather = s32[4,1,768]{2,1,0:T(1,128)S(1)} all-gather(s32[1,1,768]{2,1,0:T(1,128)S(1)} %reshape.22), channel_id=1, replica_groups=mesh['dp'=8,'neg'=4] {'neg'}, dimensions={0}, use_global_device_ids=true | all-gather | bytes 15360 | tf_op jit(solution)/shard_map/all_gather | solution.py:48
  14.9 1.2 slice.18
  16.1 0.7 slice_bitcast_fusion
  16.8 0.1 compare_reduce_fusion
  16.9 1.3 multiply_reduce_fusion
  18.2 13.7 %all-gather.5.cloned.1.call-done = bf16[3072,256]{1,0:T(8,128)(2,1)} async-done(((bf16[768,256]{1,0:T(8,128)(2,1)}), bf16[3072,256]{1,0:T(8,128)(2,1)}) %all-gather.5.cloned.1.call-update) | async-done | bytes 1572880 | tf_op jit(solution)/shard_map/all_gather | solution.py:47
  31.9 0.0 copy-start.1
  31.9 59.9 %while.24 = (s32[]{:T(128)}, f32[6,512]{1,0:T(8,128)S(1)}, f32[6,512]{1,0:T(8,128)S(1)}, s32[6,512]{1,0:T(8,128)S(1)}, s32[8192]{0:T(1024)}, /*index=5*/bf16[6,5...) while((s32[]{:T(128)}, f32[6,512]{1,0:T(8,128)S(1)}, f32[6,512]{1,0:T(8,128)S(1)}, ...), condition=%wide.region_4.5_spmd, body=%wide.region_1.4_spmd.sunk | while | flops 2185231360 | bytes 38230660 | solution.py:57
  31.9 0.0 copy-start
  31.9 5.1 %fusion.16 = (f32[512]{0:T(512)S(1)}, f32[512,8192]{1,0:T(8,128)S(1)}) fusion(s32[8192]{0:T(1024)} %get-tuple-element.215, s32[512]{0:T(512)S(1)} %bitcast.44, bf16[8192,256]{1,0:T(8,128)(2,1)} %get-tuple-element.217, bf16[6,512,256]{2,1,0:T(8,128)(2,1)} %get-tuple-element.216, s32[]{:T(128)} %get-tuple-element.202), kind=kOutput, calls=%fused_computation.2.clone.1 | convolution fusion | flops 2164260352 | bytes 21271040 | tf_op jit(solution)/shard_map/while/body/eval_jaxpr/dot_general | solution.py:21
  37.1 0.0 copy-done
  37.1 4.6 %fusion.17 = f32[512]{0:T(512)S(1)} fusion(f32[512,8192]{1,0:T(8,128)S(1)} %get-tuple-element.183, f32[512]{0:T(512)S(1)} %get-tuple-element.182, s32[8192]{0:T(1024)S(1)} %copy-done, s32[512]{0:T(512)S(1)} %bitcast.45), kind=kLoop, calls=%fused_computation.3.clone.1 | loop fusion | flops 20971008 | bytes 16816128 | tf_op jit(solution)/shard_map/while/body/eval_jaxpr/reduce_sum | solution.py:26
  41.7 0.1 dynamic_update_slice.10
  41.8 0.1 dynamic_update_slice.9
  41.9 0.0 copy-start
  41.9 5.1 %fusion.16 = (f32[512]{0:T(512)S(1)}, f32[512,8192]{1,0:T(8,128)S(1)}) fusion(s32[8192]{0:T(1024)} %get-tuple-element.215, s32[512]{0:T(512)S(1)} %bitcast.44, bf16[8192,256]{1,0:T(8,128)(2,1)} %get-tuple-element.217, bf16[6,512,256]{2,1,0:T(8,128)(2,1)} %get-tuple-element.216, s32[]{:T(128)} %get-tuple-element.202), kind=kOutput, calls=%fused_computation.2.clone.1 | convolution fusion | flops 2164260352 | bytes 21271040 | tf_op jit(solution)/shard_map/while/body/eval_jaxpr/dot_general | solution.py:21
  47.1 0.0 copy-done
  47.1 4.6 %fusion.17 = f32[512]{0:T(512)S(1)} fusion(f32[512,8192]{1,0:T(8,128)S(1)} %get-tuple-element.183, f32[512]{0:T(512)S(1)} %get-tuple-element.182, s32[8192]{0:T(1024)S(1)} %copy-done, s32[512]{0:T(512)S(1)} %bitcast.45), kind=kLoop, calls=%fused_computation.3.clone.1 | loop fusion | flops 20971008 | bytes 16816128 | tf_op jit(solution)/shard_map/while/body/eval_jaxpr/reduce_sum | solution.py:26
  51.7 0.1 dynamic_update_slice.10
  51.8 0.1 dynamic_update_slice.9
  51.9 0.0 copy-start
  51.9 5.1 %fusion.16 = (f32[512]{0:T(512)S(1)}, f32[512,8192]{1,0:T(8,128)S(1)}) fusion(s32[8192]{0:T(1024)} %get-tuple-element.215, s32[512]{0:T(512)S(1)} %bitcast.44, bf16[8192,256]{1,0:T(8,128)(2,1)} %get-tuple-element.217, bf16[6,512,256]{2,1,0:T(8,128)(2,1)} %get-tuple-element.216, s32[]{:T(128)} %get-tuple-element.202), kind=kOutput, calls=%fused_computation.2.clone.1 | convolution fusion | flops 2164260352 | bytes 21271040 | tf_op jit(solution)/shard_map/while/body/eval_jaxpr/dot_general | solution.py:21
  57.1 0.0 copy-done
  57.1 4.6 %fusion.17 = f32[512]{0:T(512)S(1)} fusion(f32[512,8192]{1,0:T(8,128)S(1)} %get-tuple-element.183, f32[512]{0:T(512)S(1)} %get-tuple-element.182, s32[8192]{0:T(1024)S(1)} %copy-done, s32[512]{0:T(512)S(1)} %bitcast.45), kind=kLoop, calls=%fused_computation.3.clone.1 | loop fusion | flops 20971008 | bytes 16816128 | tf_op jit(solution)/shard_map/while/body/eval_jaxpr/reduce_sum | solution.py:26
  61.7 0.1 dynamic_update_slice.10
  61.8 0.1 dynamic_update_slice.9
  61.9 0.0 copy-start
  61.9 5.1 %fusion.16 = (f32[512]{0:T(512)S(1)}, f32[512,8192]{1,0:T(8,128)S(1)}) fusion(s32[8192]{0:T(1024)} %get-tuple-element.215, s32[512]{0:T(512)S(1)} %bitcast.44, bf16[8192,256]{1,0:T(8,128)(2,1)} %get-tuple-element.217, bf16[6,512,256]{2,1,0:T(8,128)(2,1)} %get-tuple-element.216, s32[]{:T(128)} %get-tuple-element.202), kind=kOutput, calls=%fused_computation.2.clone.1 | convolution fusion | flops 2164260352 | bytes 21271040 | tf_op jit(solution)/shard_map/while/body/eval_jaxpr/dot_general | solution.py:21
  67.0 0.0 copy-done
  67.1 4.6 %fusion.17 = f32[512]{0:T(512)S(1)} fusion(f32[512,8192]{1,0:T(8,128)S(1)} %get-tuple-element.183, f32[512]{0:T(512)S(1)} %get-tuple-element.182, s32[8192]{0:T(1024)S(1)} %copy-done, s32[512]{0:T(512)S(1)} %bitcast.45), kind=kLoop, calls=%fused_computation.3.clone.1 | loop fusion | flops 20971008 | bytes 16816128 | tf_op jit(solution)/shard_map/while/body/eval_jaxpr/reduce_sum | solution.py:26
  71.7 0.1 dynamic_update_slice.10
  71.8 0.1 dynamic_update_slice.9
  71.9 0.0 copy-start
  71.9 5.1 %fusion.16 = (f32[512]{0:T(512)S(1)}, f32[512,8192]{1,0:T(8,128)S(1)}) fusion(s32[8192]{0:T(1024)} %get-tuple-element.215, s32[512]{0:T(512)S(1)} %bitcast.44, bf16[8192,256]{1,0:T(8,128)(2,1)} %get-tuple-element.217, bf16[6,512,256]{2,1,0:T(8,128)(2,1)} %get-tuple-element.216, s32[]{:T(128)} %get-tuple-element.202), kind=kOutput, calls=%fused_computation.2.clone.1 | convolution fusion | flops 2164260352 | bytes 21271040 | tf_op jit(solution)/shard_map/while/body/eval_jaxpr/dot_general | solution.py:21
  77.0 0.0 copy-done
  77.0 4.6 %fusion.17 = f32[512]{0:T(512)S(1)} fusion(f32[512,8192]{1,0:T(8,128)S(1)} %get-tuple-element.183, f32[512]{0:T(512)S(1)} %get-tuple-element.182, s32[8192]{0:T(1024)S(1)} %copy-done, s32[512]{0:T(512)S(1)} %bitcast.45), kind=kLoop, calls=%fused_computation.3.clone.1 | loop fusion | flops 20971008 | bytes 16816128 | tf_op jit(solution)/shard_map/while/body/eval_jaxpr/reduce_sum | solution.py:26
  81.7 0.1 dynamic_update_slice.10
  81.8 0.1 dynamic_update_slice.9
  81.8 0.0 copy-start
  81.9 5.1 %fusion.16 = (f32[512]{0:T(512)S(1)}, f32[512,8192]{1,0:T(8,128)S(1)}) fusion(s32[8192]{0:T(1024)} %get-tuple-element.215, s32[512]{0:T(512)S(1)} %bitcast.44, bf16[8192,256]{1,0:T(8,128)(2,1)} %get-tuple-element.217, bf16[6,512,256]{2,1,0:T(8,128)(2,1)} %get-tuple-element.216, s32[]{:T(128)} %get-tuple-element.202), kind=kOutput, calls=%fused_computation.2.clone.1 | convolution fusion | flops 2164260352 | bytes 21271040 | tf_op jit(solution)/shard_map/while/body/eval_jaxpr/dot_general | solution.py:21
  87.0 0.0 copy-done
  87.0 4.6 %fusion.17 = f32[512]{0:T(512)S(1)} fusion(f32[512,8192]{1,0:T(8,128)S(1)} %get-tuple-element.183, f32[512]{0:T(512)S(1)} %get-tuple-element.182, s32[8192]{0:T(1024)S(1)} %copy-done, s32[512]{0:T(512)S(1)} %bitcast.45), kind=kLoop, calls=%fused_computation.3.clone.1 | loop fusion | flops 20971008 | bytes 16816128 | tf_op jit(solution)/shard_map/while/body/eval_jaxpr/reduce_sum | solution.py:26
  91.7 0.1 dynamic_update_slice.10
  91.7 0.1 dynamic_update_slice.9
  91.8 5.2 %all-gather.2 = f32[4,1,3072]{2,1,0:T(1,128)S(1)} all-gather(f32[1,1,3072]{2,1,0:T(1,128)S(1)} %reshape.26), channel_id=1, replica_groups=mesh['dp'=8,'neg'=4] {'neg'}, dimensions={0}, use_global_device_ids=true | all-gather | bytes 61440 | tf_op jit(solution)/shard_map/all_gather | solution.py:12
  97.1 5.2 %all-gather.1 = f32[4,1,3072]{2,1,0:T(1,128)S(1)} all-gather(f32[1,1,3072]{2,1,0:T(1,128)S(1)} %reshape.24), channel_id=1, replica_groups=mesh['dp'=8,'neg'=4] {'neg'}, dimensions={0}, use_global_device_ids=true | all-gather | bytes 61440 | tf_op jit(solution)/shard_map/all_gather | solution.py:12
  102.4 0.2 while.25
  102.6 0.0 copy-done.1
  102.6 2.0 %select_reduce_fusion = (f32[]{:T(128)}, f32[]{:T(128)}, f32[768]{0:T(1024)}) fusion(s32[768]{0:T(1024)S(1)} %copy-done.1, pred[768]{0:T(1024)(128)(4,1)S(1)} %compare_reduce_fusion, s32[]{:T(128)} %bitcast.6, s32[]{:T(128)S(6)} %mul.31, f32[3072]{0:T(1024)S(1)} %get-tuple-element.71, s32[]{:T(128)S(6)} %select_n.15, f32[768]{0:T(1024)S(1)} %multiply_reduce_fusion, ...), kind=kLoop, calls=%fused_computation.16 | loop fusion | flops 13822 | bytes 16148 | tf_op jit(solution)/shard_map/reduce_sum | solution.py:73
  104.6 39.5 %all-reduce = (f32[]{:T(128)}, f32[]{:T(128)}) all-reduce(f32[]{:T(128)} %get-tuple-element.73, f32[]{:T(128)} %get-tuple-element.72), channel_id=1, replica_groups=mesh['dp'=8,'neg'=4] {'dp','neg'}, use_global_device_ids=true, to_apply=%region_9.10 | all-reduce | flops 2 | bytes 16 | tf_op jit(solution)/shard_map/psum | solution.py:73
  (25 shorter events, 0.3 us)
Async XLA Ops:
  7.2 24.8 %all-gather.5.cloned.1.call-start = ((), (), s32[]{:S(2)}) async-start(), calls=%async_computation | async-start | bytes 1966080 | tf_op jit(solution)/shard_map/all_gather | solution.py:47
  31.9 70.7 %copy-start.1 = (s32[768]{0:T(1024)S(1)}, s32[768]{0:T(1024)}, u32[]{:S(2)}) copy-start(s32[768]{0:T(1024)} %param.14) | copy-start | bytes 9220
  31.9 5.2 %copy-start = (s32[8192]{0:T(1024)S(1)}, s32[8192]{0:T(1024)}, u32[]{:S(2)}) copy-start(s32[8192]{0:T(1024)} %get-tuple-element.215) | copy-start | bytes 98308 | tf_op jit(solution)/shard_map/while
  41.9 5.2 %copy-start = (s32[8192]{0:T(1024)S(1)}, s32[8192]{0:T(1024)}, u32[]{:S(2)}) copy-start(s32[8192]{0:T(1024)} %get-tuple-element.215) | copy-start | bytes 98308 | tf_op jit(solution)/shard_map/while
  51.9 5.2 %copy-start = (s32[8192]{0:T(1024)S(1)}, s32[8192]{0:T(1024)}, u32[]{:S(2)}) copy-start(s32[8192]{0:T(1024)} %get-tuple-element.215) | copy-start | bytes 98308 | tf_op jit(solution)/shard_map/while
  61.9 5.2 %copy-start = (s32[8192]{0:T(1024)S(1)}, s32[8192]{0:T(1024)}, u32[]{:S(2)}) copy-start(s32[8192]{0:T(1024)} %get-tuple-element.215) | copy-start | bytes 98308 | tf_op jit(solution)/shard_map/while
  71.9 5.2 %copy-start = (s32[8192]{0:T(1024)S(1)}, s32[8192]{0:T(1024)}, u32[]{:S(2)}) copy-start(s32[8192]{0:T(1024)} %get-tuple-element.215) | copy-start | bytes 98308 | tf_op jit(solution)/shard_map/while
  81.8 5.2 %copy-start = (s32[8192]{0:T(1024)S(1)}, s32[8192]{0:T(1024)}, u32[]{:S(2)}) copy-start(s32[8192]{0:T(1024)} %get-tuple-element.215) | copy-start | bytes 98308 | tf_op jit(solution)/shard_map/while
Sparse Core Ops, SparseCore 0:
  9.5 22.3 all-gather.4
where the time goes:
time: 154 us; the launch traced here: 153 us
  blocking collectives  56.2 us (36%)
  other arithmetic  31.4 us (20%)
  matrix products  30.9 us (20%)
  between operations  16.6 us (11%)
  waiting for transfers between devices  14.4 us (9%)
  local copies, waits for them, and re-layouts  3.64 us (2%)
    psum x1, blocking collectives, shards(): total, count = lax.psum((weighted, jnp.sum(live_weight)), ('dp', 'neg'))  39.5 us
    dot_general x6, matrix products, shard_partials(): lax.dot_general(rows, columns, (((1,), (1,)), ((), ())), preferred_elemen...  30.9 us
    reduce_sum x6, other arithmetic, shard_partials(): jnp.sum(jnp.where(hit, 0.0, jnp.exp(logits - peak[:, None])), axis=1)  27.9 us
    all_gather x1, waiting for transfers between devices, shards(): rows = lax.all_gather(user_embed, 'neg', axis=0, tiled=True)  13.7 us
    all_gather x2, blocking collectives, merged(): pieces = jax.tree.map(lambda part: lax.all_gather(part, axis), value)  10.4 us
    all_gather x1, blocking collectives, shards(): row_ids = lax.all_gather(positive_ids, 'neg', axis=0, tiled=True)  6.2 us
  transfers between devices with their start and end apart: 1, of which 1 were waited for; matrix products, arithmetic and copies ran while one was open for 3% of the time, Pallas kernels for 0%

commit v1 on v0

v1 whole, which is shorter than its diff:
```python
import functools
import math

import jax
import jax.numpy as jnp
from jax import lax
from jax.experimental import pallas as pl
from jax.experimental.pallas import tpu as pltpu
from jax.sharding import PartitionSpec as P

LANES = 128
TILE = 256
BLOCK = 512
ID_ROWS = 16
BATCH = 16
LOG2E = math.log2(math.e)
FLOOR = -1e30
HIGHEST = 2.0**126
LOWEST = 2.0**-90
CONTRACT = (((1,), (1,)), ((), ()))
VMEM = pl.BlockSpec(memory_space=pltpu.VMEM)
SMEM = pl.BlockSpec(memory_space=pltpu.SMEM)


def pack_kernel(users, places, out):
    tokens = users.shape[0]
    tiles = tokens // TILE
    out[0:tokens, :] = users[...]
    ids = places[...]
    lines = []
    for digit in (ids & 127, (ids >> 7) & 127, ids >> 14):
        digit = digit.astype(jnp.float32)
        for tile in range(tiles):
            lines.append(
                jnp.concatenate(
                    [digit[2 * tile : 2 * tile + 1], digit[2 * tile + 1 : 2 * tile + 2]], axis=1
                )
            )
    lines.append(jnp.zeros((ID_ROWS - len(lines), TILE), jnp.float32))
    out[tokens:, :] = jnp.concatenate(lines, axis=0).astype(out.dtype)


def tile_ids(pack, tile):
    tokens = pack.shape[0] - ID_ROWS
    tiles = tokens // TILE
    digits = pack[tokens:, :].astype(jnp.float32)
    rows = [digits[d * tiles + tile : d * tiles + tile + 1] for d in range(3)]
    return rows[0] + 128.0 * rows[1] + 16384.0 * rows[2]


def sum_pack(scale2, pack, negs, id_rows, out, first):
    tokens = pack.shape[0] - ID_ROWS
    number = negs.shape[0]
    tiles = tokens // TILE
    wanted = [
        jnp.broadcast_to(tile_ids(pack, tile), (8, TILE)).astype(jnp.int32) for tile in range(tiles)
    ]
    totals = [jnp.zeros((8, LANES), jnp.float32) for _ in range(2 * tiles)]
    for start in range(0, number, BLOCK):
        size = min(BLOCK, number - start)
        block = negs[pl.ds(start, size), :]
        others = [
            jnp.broadcast_to(id_rows[row : row + 1, :], (LANES, LANES)).T
            for row in range(start // LANES, (start + size) // LANES)
        ]
        others = jnp.concatenate(others, axis=0).reshape(size // 8, 8, LANES)
        for tile in range(tiles):
            users = pack[tile * TILE : (tile + 1) * TILE, :]
            logit = lax.dot_general(block, users, CONTRACT, preferred_element_type=jnp.float32)
            grown = jnp.exp2(logit * scale2)
            for half in range(2):
                lanes = slice(half * LANES, (half + 1) * LANES)
                part = grown[:, lanes].reshape(size // 8, 8, LANES)
                part = jnp.where(others == wanted[tile][None, :, lanes], 0.0, part)
                totals[2 * tile + half] = totals[2 * tile + half] + part.sum(0)
    for row in range(2 * tiles):
        out[first + row : first + row + 1, :] = jnp.sum(totals[row], axis=0, keepdims=True)


def sums_kernel(scale2, count, *refs):
    packs, (negs, id_rows, out) = refs[:count], refs[count:]
    rows = (packs[0].shape[0] - ID_ROWS) // LANES
    for k, pack in enumerate(packs):
        sum_pack(scale2, pack, negs, id_rows, out, k * rows)


def side_kernel(scale2, me, offsets, pack, targets, weights, out):
    tokens = targets.shape[0]
    rows = tokens // LANES
    product = pack[0:tokens, :].astype(jnp.float32) * targets[...].astype(jnp.float32)
    high = product.astype(jnp.bfloat16)
    low = (product - high.astype(jnp.float32)).astype(jnp.bfloat16)
    ones = jnp.ones((16, product.shape[1]), jnp.bfloat16)
    positive = lax.dot_general(
        ones, high, CONTRACT, preferred_element_type=jnp.float32
    ) + lax.dot_general(ones, low, CONTRACT, preferred_element_type=jnp.float32)
    positive = positive * scale2
    for row in range(rows):
        out[row : row + 1, :] = positive[0:1, row * LANES : (row + 1) * LANES]
    line = lax.broadcasted_iota(jnp.int32, (rows, LANES), 0)
    lane = lax.broadcasted_iota(jnp.int32, (rows, LANES), 1)
    position = me[0] * tokens + line * LANES + lane
    users = offsets.shape[1]
    live = position < offsets[0, users - 1]
    for user in range(1, users):
        live = live & (position + 1 != offsets[0, user])
    out[rows:, :] = jnp.where(live, weights[...], 0).astype(jnp.float32)


def last_kernel(scale2, members, *refs):
    packs = refs[:members]
    negs, id_rows, *rest = refs[members:]
    early, side, out, sums, chosen, picked, mine, logits, values = (
        rest[: members - 2],
        *rest[members - 2 :],
    )
    tokens = packs[0].shape[0] - ID_ROWS
    number = negs.shape[0]
    rows = tokens // LANES
    lines = members * rows
    first = 0
    for share in early:
        sums[first : first + share.shape[0], :] = share[...]
        first += share.shape[0]
    sum_pack(scale2, packs[-1], negs, id_rows, sums, first)
    total = sums[...]
    good = (total < HIGHEST) & (total > LOWEST)
    out[0:lines, :] = jnp.log2(jnp.where(good, total, 1.0))
    out[lines:, :] = side[...]
    bad = jnp.where(good, 0.0, 1.0)

    @pl.when(jnp.max(bad) > 0.0)
    def _():
        place = lax.broadcasted_iota(jnp.int32, (lines, LANES), 0) * LANES
        place = (place + lax.broadcasted_iota(jnp.int32, (lines, LANES), 1)).astype(jnp.float32)
        beyond = float(lines * LANES)
        sums[...] = jnp.where(good, beyond, place)
        wanted = []
        for pack in packs:
            for tile in range(tokens // TILE):
                row = tile_ids(pack, tile)
                wanted += [row[:, :LANES], row[:, LANES:]]
        wanted = jnp.concatenate(wanted, axis=0)
        picked[...] = jnp.zeros_like(picked)
        mine[...] = jnp.zeros_like(mine)
        count = jnp.sum(bad).astype(jnp.int32)

        def rescue(b, _):
            here = jnp.minimum(count - b * BATCH, BATCH)

            def pick(i, _):
                left = sums[...]
                found = jnp.min(left)
                at = found.astype(jnp.int32)
                chosen[i] = at
                sums[...] = jnp.where(left == found, beyond, left)
                number_of = jnp.sum(jnp.where(place == found, wanted, 0.0))
                mine[pl.ds(i, 1), :] = jnp.full((1, LANES), number_of, jnp.float32)
                inside = lax.rem(at, tokens)
                line = lax.rem(inside, 16)
                start = pl.multiple_of(inside - line, 16)
                for k, pack in enumerate(packs):

                    @pl.when(at // tokens == k)
                    def _(pack=pack):
                        group = pack[pl.ds(start, 16), :].astype(jnp.float32)
                        at_line = lax.broadcasted_iota(jnp.int32, group.shape, 0) == line
                        picked[pl.ds(i, 1), :] = jnp.sum(
                            jnp.where(at_line, group, 0.0), axis=0, keepdims=True
                        )

                return 0

            lax.fori_loop(0, here, pick, 0)
            users = picked[...].astype(jnp.bfloat16)
            ids = mine[...]
            peak = jnp.full((BATCH, LANES), FLOOR, jnp.float32)
            for start in range(0, number, 1024):
                size = min(1024, number - start)
                part = lax.dot_general(
                    users, negs[pl.ds(start, size), :], CONTRACT, preferred_element_type=jnp.float32
                )
                part = part * scale2
                for k in range(size // LANES):
                    row = start // LANES + k
                    other = id_rows[row : row + 1, :].astype(jnp.float32)
                    piece = jnp.where(other == ids, FLOOR, part[:, k * LANES : (k + 1) * LANES])
                    logits[row] = piece
                    peak = jnp.maximum(peak, piece)
            peak = jnp.max(peak, axis=1, keepdims=True)
            amount = jnp.zeros((BATCH, LANES), jnp.float32)
            for row in range(number // LANES):
                piece = logits[row]
                amount = amount + jnp.where(piece > 0.5 * FLOOR, jnp.exp2(piece - peak), 0.0)
            amount = jnp.sum(amount, axis=1, keepdims=True)
            some = amount > 0.0
            value = jnp.where(some, peak + jnp.log2(jnp.where(some, amount, 1.0)), FLOOR)
            values[...] = jnp.broadcast_to(value, (BATCH, LANES))

            def put(i, _):
                at = chosen[i].astype(jnp.float32)
                out[0:lines, :] = jnp.where(place == at, values[pl.ds(i, 1), :], out[0:lines, :])
                return 0

            lax.fori_loop(0, here, put, 0)
            return 0

        lax.fori_loop(0, (count + BATCH - 1) // BATCH, rescue, 0)


def finish_kernel(members, rows, me, gathered, loss_out, totals_out):
    weighted = jnp.zeros((rows, LANES), jnp.float32)
    counted = jnp.zeros((rows, LANES), jnp.float32)
    own = jnp.zeros((rows, LANES), jnp.float32)
    for owner in range(members):
        positive = gathered[owner, members * rows : (members + 1) * rows, :]
        weight = gathered[owner, (members + 1) * rows : (members + 2) * rows, :]
        shares = [
            gathered[k, (owner ^ k) * rows : ((owner ^ k) + 1) * rows, :] for k in range(members)
        ]
        peak = positive
        for share in shares:
            peak = jnp.maximum(peak, share)
        total = jnp.exp2(positive - peak)
        for share in shares:
            total = total + jnp.exp2(share - peak)
        loss = (peak - positive + jnp.log2(total)) * (1.0 / LOG2E)
        loss = jnp.where(weight > 0.0, loss, 0.0)
        weighted = weighted + weight * loss
        counted = counted + weight
        own = jnp.where(me[0] == owner, loss, own)
    loss_out[...] = own
    first = jnp.sum(weighted, axis=0, keepdims=True)
    second = jnp.sum(counted, axis=0, keepdims=True)
    line = lax.broadcasted_iota(jnp.int32, (8, LANES), 0)
    totals_out[...] = jnp.where(line == 0, first, jnp.where(line == 1, second, 0.0))


def call(kernel, shapes, *args, flags=None, cost=None, scratch=(), smem=0, limit=16):
    return pl.pallas_call(
        kernel,
        out_shape=shapes,
        in_specs=[SMEM] * smem + [VMEM] * (len(args) - smem),
        out_specs=jax.tree.map(lambda _: VMEM, shapes),
        scratch_shapes=list(scratch),
        compiler_params=pltpu.CompilerParams(vmem_limit_bytes=limit * 2**20, flags=flags),
        cost_estimate=cost,
    )(*args)


def exchanged(value, axis, size, mask):
    return lax.ppermute(value, axis, [(i, i ^ mask) for i in range(size)])


def shards(
    dp,
    members,
    user_embed,
    positive_embed,
    positive_ids,
    token_weights,
    offsets,
    negative_embed,
    negative_ids,
):
    tokens, width = user_embed.shape
    number = negative_embed.shape[0]
    rows = tokens // LANES
    scale2 = 3.0 / math.sqrt(width) * LOG2E
    me = lax.axis_index("neg").reshape(1).astype(jnp.int32)
    id_rows = negative_ids.reshape(number // LANES, LANES)
    f32 = lambda *shape: jax.ShapeDtypeStruct(shape, jnp.float32)

    def cost(count):
        return pl.CostEstimate(
            flops=2 * count * tokens * number * width,
            bytes_accessed=number * width * 2,
            transcendentals=count * tokens * number,
        )

    pack = call(
        pack_kernel,
        jax.ShapeDtypeStruct((tokens + ID_ROWS, width), user_embed.dtype),
        user_embed,
        positive_ids.reshape(rows, LANES),
        cost=cost(1),
    )
    packs = [pack, exchanged(pack, "neg", members, 1)]
    for mask in [2**k for k in range(1, members.bit_length() - 1)]:
        packs += [exchanged(pack, "neg", members, mask)] + [None] * (mask - 1)
    side = call(
        functools.partial(side_kernel, scale2),
        f32(2 * rows, LANES),
        me,
        offsets,
        pack,
        positive_embed,
        token_weights.reshape(rows, LANES),
        smem=2,
        cost=cost(1),
    )
    own, side = lax.optimization_barrier((pack, side))
    early = [
        call(
            functools.partial(sums_kernel, scale2, 2),
            f32(2 * rows, LANES),
            own,
            packs[1],
            negative_embed,
            id_rows,
            cost=cost(2),
        )
    ]
    for mask in range(2, members):
        if packs[mask] is None:
            low = mask & -mask
            source, early[0] = lax.optimization_barrier((packs[mask ^ low], early[0]))
            packs[mask] = exchanged(source, "neg", members, low)
    for mask in range(2, members - 1):
        early.append(
            call(
                functools.partial(sums_kernel, scale2, 1),
                f32(rows, LANES),
                packs[mask],
                negative_embed,
                id_rows,
                cost=cost(1),
            )
        )
    lines = members * rows
    payload = call(
        functools.partial(last_kernel, scale2, members),
        f32(lines + 2 * rows, LANES),
        *packs,
        negative_embed,
        id_rows,
        *early,
        side,
        cost=cost(1),
        scratch=[
            pltpu.VMEM((lines, LANES), jnp.float32),
            pltpu.SMEM((BATCH,), jnp.int32),
            pltpu.VMEM((BATCH, width), jnp.float32),
            pltpu.VMEM((BATCH, LANES), jnp.float32),
            pltpu.VMEM((number // LANES, BATCH, LANES), jnp.float32),
            pltpu.VMEM((BATCH, LANES), jnp.float32),
        ],
    )
    gathered = lax.all_gather(payload, "neg", axis=0)
    loss, totals = call(
        functools.partial(finish_kernel, members, rows),
        (f32(rows, LANES), f32(8, LANES)),
        me,
        gathered,
        smem=1,
    )
    mask = 1
    while mask < dp:
        totals = totals + exchanged(totals, "dp", dp, mask)
        mask *= 2
    mean = jnp.sum(totals[0]) / jnp.sum(totals[1])
    return (loss.reshape(tokens), mean)


def solution(mesh):
    dp, members = mesh.shape["dp"], mesh.shape["neg"]
    in_specs = (
        P(("dp", "neg"), None),
        P(("dp", "neg"), None),
        P(("dp", "neg")),
        P(("dp", "neg")),
        P("dp", None),
        P("neg", None),
        P("neg"),
    )
    out_specs = (P(("dp", "neg")), P())
    return jax.shard_map(
        functools.partial(shards, dp, members),
        mesh=mesh,
        in_specs=in_specs,
        out_specs=out_specs,
        check_vma=False,
    )
```

time: 154 us -> 51.8 us (0.34)
  blocking collectives: 56.2 us -> 5.28 us
  matrix products: 30.9 us -> 0 us
  other arithmetic: 31.4 us -> 0.67 us
  Pallas kernels: 0 us -> 24.6 us
  between operations: 16.6 us -> 3.15 us
  starting transfers between devices: 0.04 us -> 7.12 us
  waiting for transfers between devices: 14.4 us -> 7.94 us
    psum x1 -> x0, blocking collectives: 39.5 us -> none  [shards(): total, count = lax.psum((weighted, jnp.sum(live_weight)), ('dp', 'neg'))]
    dot_general x6 -> x0, matrix products: 30.9 us -> none  [shard_partials(): lax.dot_general(rows, columns, (((1,), (1,)), ((), ())), preferred_elemen...]
    reduce_sum x8 -> x1, other arithmetic: 31.2 us -> 0.66 us  [shards(): mean = jnp.sum(totals[0]) / jnp.sum(totals[1])]
    pallas_call x0 -> x6, Pallas kernels: none -> 24.6 us  [call(): pl.pallas_call(kernel, out_shape=shapes, in_specs=[SMEM] * smem + [VMEM]...]
    all_gather x1 -> x0, waiting for transfers between devices: 13.7 us -> none  [shards(): rows = lax.all_gather(user_embed, 'neg', axis=0, tiled=True)]
    all_gather x3 -> x1, blocking collectives: 16.6 us -> 5.28 us  [shards(): gathered = lax.all_gather(payload, 'neg', axis=0)]
    ppermute x0 -> x6, waiting for transfers between devices: none -> 7.94 us  [exchanged(): return lax.ppermute(value, axis, [(i, i ^ mask) for i in range(size)])]
    ppermute x0 -> x6, starting transfers between devices: none -> 7.12 us  [exchanged(): return lax.ppermute(value, axis, [(i, i ^ mask) for i in range(size)])]
  transfers between devices with their start and end apart: 1 -> 6, of which waited for: 1 -> 3; matrix products, arithmetic and copies ran while one was open for 3% -> 0% of each run, Pallas kernels for 0% -> 31%
where the time goes in v1:
time: 51.8 us; the launch traced here: 51.7 us
  Pallas kernels  24.6 us (47%)
  waiting for transfers between devices  7.94 us (15%)
  starting transfers between devices  7.12 us (14%)
  blocking collectives  5.28 us (10%)
  between operations  3.15 us (6%)
  local copies, waits for them, and re-layouts  2.96 us (6%)
  other arithmetic  0.67 us (1%)
    pallas_call x6, Pallas kernels, call(): pl.pallas_call(kernel, out_shape=shapes, in_specs=[SMEM] * smem + [VMEM]...  24.6 us
    ppermute x6, waiting for transfers between devices, exchanged(): return lax.ppermute(value, axis, [(i, i ^ mask) for i in range(size)])  7.94 us
    ppermute x6, starting transfers between devices, exchanged(): return lax.ppermute(value, axis, [(i, i ^ mask) for i in range(size)])  7.12 us
    all_gather x1, blocking collectives, shards(): gathered = lax.all_gather(payload, 'neg', axis=0)  5.28 us
    unnamed x14, local copies, waits for them, and re-layouts  2.96 us
  transfers between devices with their start and end apart: 6, of which 3 were waited for; matrix products, arithmetic and copies ran while one was open for 0% of the time, Pallas kernels for 31%

profile of v1, /device:TPU:0, one launch (start us, length us, event | category | flops | bytes accessed | tf_op | source)
XLA Modules:
  0.0 51.7 jit_solution(10180857363317032505)
XLA Ops:
  0.6 0.0 copy-start.1
  0.6 1.0 %copy-done.1 = bf16[768,256]{1,0:T(8,128)(2,1)S(1)} copy-done((bf16[768,256]{1,0:T(8,128)(2,1)S(1)}, bf16[768,256]{1,0:T(8,128)(2,1)}, u32[]{:S(2)}) %copy-start.1) | copy-done | bytes 393240
  1.6 0.0 copy-start.4
  1.6 0.7 %copy-done.4 = s32[768]{0:T(1024)S(1)} copy-done((s32[768]{0:T(1024)S(1)}, s32[768]{0:T(1024)}, u32[]{:S(2)}) %copy-start.4) | copy-done | bytes 3096
  2.3 0.0 copy-start.2
  2.3 0.0 copy-start.5
  2.3 0.0 copy-start.6
  2.4 0.6 %collective-permute-start = (bf16[784,256]{1,0:T(8,128)(2,1)S(1)}, bf16[784,256]{1,0:T(8,128)(2,1)S(1)}, u32[]{:S(2)}, u32[]{:S(2)}) collective-permute-start(bf16[784,256]{1,0:T(8,128)(2,1)S(1)} %shard_map.86.pack.refs_0_), channel_id=1, source_target_pairs={{0,1},{1,0},{2,3},{3,2},{4,5},{5,4},{6,7},{7,6},{8,9},{9,8},{10,11... | collective-permute-start | bytes 1204232 | tf_op jit(solution)/shard_map/ppermute | solution.py:252
  2.9 2.6 %collective-permute-start.1 = (bf16[784,256]{1,0:T(8,128)(2,1)S(1)}, bf16[784,256]{1,0:T(8,128)(2,1)S(1)}, u32[]{:S(2)}, u32[]{:S(2)}) collective-permute-start(bf16[784,256]{1,0:T(8,128)(2,1)S(1)} %shard_map.86.pack.refs_0_), channel_id=1, source_target_pairs={{0,2},{1,3},{2,0},{3,1},{4,6},{5,7},{6,4},{7,5},{8,10},{9,11},{10,... | collective-permute-start | bytes 1204232 | tf_op jit(solution)/shard_map/ppermute | solution.py:252
  5.5 0.0 copy-done.2
  5.5 0.0 copy-done.5
  5.5 0.0 copy-done.6
  5.5 0.0 copy-start
  5.5 0.0 copy-start.3
  5.5 0.9 %shard_map.87.refs_8_ = f32[12,128]{1,0:T(8,128)S(1)} custom-call(s32[1]{0:T(128)} %bitcast.me, s32[1,25]{1,0:T(1,128)S(1)} %copy-done.6, bf16[784,256]{1,0:T(8,128)(2,1)S(1)} %shard_map.86.pack.refs_0_, bf16[768,256]{1,0:T(8,128)(2,1)S(1)} %copy-done.2, s32[6,128]{1,0:T(8,128)S(1)} %bitcast.11), custom_call_target="tpu_custom_call" | custom-call | flops 3221225472 | bytes 4194304 | tf_op jit(solution)/shard_map/pallas_call | solution.py:240
  6.4 0.0 collective-permute-done.refs_1_
  6.4 1.3 %copy-done = bf16[8192,256]{1,0:T(8,128)(2,1)S(1)} copy-done((bf16[8192,256]{1,0:T(8,128)(2,1)S(1)}, bf16[8192,256]{1,0:T(8,128)(2,1)}, u32[]{:S(2)}) %copy-start) | copy-done | bytes 4194328
  7.7 0.0 copy-done.3
  7.7 10.0 %shard_map.88.refs_6_ = f32[12,128]{1,0:T(8,128)S(1)} custom-call(bf16[784,256]{1,0:T(8,128)(2,1)S(1)} %shard_map.86.pack.refs_0_, bf16[784,256]{1,0:T(8,128)(2,1)S(1)} %collective-permute-done.refs_1_, bf16[8192,256]{1,0:T(8,128)(2,1)S(1)} %copy-done, s32[64,128]{1,0:T(8,128)S(1)} %bitcast.7), custom_call_target="tpu_custom_call" | custom-call | flops 6442450944 | bytes 4194304 | tf_op jit(solution)/shard_map/pallas_call | solution.py:240
  17.7 0.0 collective-permute-done.1.refs_0_.refs_2_
  17.7 0.2 collective-permute-start.2
  17.9 5.2 %shard_map.89.refs_7_ = f32[6,128]{1,0:T(8,128)S(1)} custom-call(bf16[784,256]{1,0:T(8,128)(2,1)S(1)} %collective-permute-done.1.refs_0_.refs_2_, bf16[8192,256]{1,0:T(8,128)(2,1)S(1)} %copy-done, s32[64,128]{1,0:T(8,128)S(1)} %bitcast.8), custom_call_target="tpu_custom_call" | custom-call | flops 3221225472 | bytes 4194304 | tf_op jit(solution)/shard_map/pallas_call | solution.py:240
  23.1 0.0 collective-permute-done.2.refs_3_
  23.1 7.8 %shard_map.90 = f32[36,128]{1,0:T(8,128)S(1)} custom-call(bf16[784,256]{1,0:T(8,128)(2,1)S(1)} %shard_map.86.pack.refs_0_, bf16[784,256]{1,0:T(8,128)(2,1)S(1)} %collective-permute-done.refs_1_, bf16[784,256]{1,0:T(8,128)(2,1)S(1)} %collective-permute-done.1.refs_0_.refs_2_, bf16[784,256]{1,0:T(8,128)(2,1)S(1)} %collective-permute-done.2.refs_3_, ...), custom_call_target="tpu_custom_call" | custom-call | flops 3221225472 | bytes 4194304 | tf_op jit(solution)/shard_map/pallas_call | solution.py:240
  30.9 5.3 %all-gather.1.gathered = f32[4,36,128]{2,1,0:T(8,128)S(1)} all-gather(f32[1,36,128]{2,1,0:T(8,128)S(1)} %bitcast.6), channel_id=2, replica_groups=mesh['dp'=8,'neg'=4] {'neg'}, dimensions={0}, use_global_device_ids=true | all-gather | bytes 92160 | tf_op jit(solution)/shard_map/all_gather | solution.py:349
  36.2 0.6 %shard_map.91 = (f32[6,128]{1,0:T(8,128)}, f32[8,128]{1,0:T(8,128)S(1)}) custom-call(s32[1]{0:T(128)} %bitcast.me, f32[4,36,128]{2,1,0:T(8,128)S(1)} %all-gather.1.gathered), custom_call_target="tpu_custom_call" | custom-call | tf_op jit(solution)/shard_map/pallas_call | solution.py:240
  36.8 0.7 %collective-permute-start.3 = (f32[8,128]{1,0:T(8,128)S(1)}, f32[8,128]{1,0:T(8,128)S(1)}, u32[]{:S(2)}, u32[]{:S(2)}) collective-permute-start(f32[8,128]{1,0:T(8,128)S(1)} %get-tuple-element.13), channel_id=1, source_target_pairs={{0,4},{4,0},{8,12},{12,8},{16,20},{20,16},{24,28},{28,24},{1,5},{5... | collective-permute-start | bytes 12296 | tf_op jit(solution)/shard_map/ppermute | solution.py:252
  37.5 2.9 %collective-permute-done.3 = f32[8,128]{1,0:T(8,128)S(1)} collective-permute-done((f32[8,128]{1,0:T(8,128)S(1)}, f32[8,128]{1,0:T(8,128)S(1)}, u32[]{:S(2)}, u32[]{:S(2)}) %collective-permute-start.3) | collective-permute-done | bytes 4128 | tf_op jit(solution)/shard_map/ppermute | solution.py:252
  40.4 0.8 %collective-permute-start.4 = (f32[8,128]{1,0:T(8,128)S(1)}, f32[8,128]{1,0:T(8,128)S(1)}, u32[]{:S(2)}, u32[]{:S(2)}) collective-permute-start(f32[8,128]{1,0:T(8,128)S(1)} %add.9), channel_id=1, source_target_pairs={{0,8},{4,12},{8,0},{12,4},{16,24},{20,28},{24,16},{28,20},{1,9},{5... | collective-permute-start | bytes 12296 | tf_op jit(solution)/shard_map/ppermute | solution.py:252
  41.2 2.8 %collective-permute-done.4 = f32[8,128]{1,0:T(8,128)S(1)} collective-permute-done((f32[8,128]{1,0:T(8,128)S(1)}, f32[8,128]{1,0:T(8,128)S(1)}, u32[]{:S(2)}, u32[]{:S(2)}) %collective-permute-start.4) | collective-permute-done | bytes 4128 | tf_op jit(solution)/shard_map/ppermute | solution.py:252
  44.1 2.3 %collective-permute-start.5 = (f32[8,128]{1,0:T(8,128)S(1)}, f32[8,128]{1,0:T(8,128)S(1)}, u32[]{:S(2)}, u32[]{:S(2)}) collective-permute-start(f32[8,128]{1,0:T(8,128)S(1)} %add.10), channel_id=1, source_target_pairs={{0,16},{4,20},{8,24},{12,28},{16,0},{20,4},{24,8},{28,12},{1,17},{... | collective-permute-start | bytes 12296 | tf_op jit(solution)/shard_map/ppermute | solution.py:252
  46.4 2.2 %collective-permute-done.5 = f32[8,128]{1,0:T(8,128)S(1)} collective-permute-done((f32[8,128]{1,0:T(8,128)S(1)}, f32[8,128]{1,0:T(8,128)S(1)}, u32[]{:S(2)}, u32[]{:S(2)}) %collective-permute-start.5) | collective-permute-done | bytes 4128 | tf_op jit(solution)/shard_map/ppermute | solution.py:252
  48.6 0.7 %slice_reduce_fusion = (f32[]{:T(128)}, f32[]{:T(128)}) fusion(f32[8,128]{1,0:T(8,128)S(1)} %add.11), kind=kLoop, calls=%fused_computation | loop fusion | flops 254 | bytes 1032 | tf_op jit(solution)/shard_map/reduce_sum | solution.py:361
  (4 shorter events, 0.0 us)
Async XLA Ops:
  0.6 1.0 %copy-start.1 = (bf16[768,256]{1,0:T(8,128)(2,1)S(1)}, bf16[768,256]{1,0:T(8,128)(2,1)}, u32[]{:S(2)}) copy-start(bf16[768,256]{1,0:T(8,128)(2,1)} %users.1) | copy-start | bytes 1179652
  1.6 0.7 %copy-start.4 = (s32[768]{0:T(1024)S(1)}, s32[768]{0:T(1024)}, u32[]{:S(2)}) copy-start(s32[768]{0:T(1024)} %param.9) | copy-start | bytes 9220
  2.3 3.2 %copy-start.2 = (bf16[768,256]{1,0:T(8,128)(2,1)S(1)}, bf16[768,256]{1,0:T(8,128)(2,1)}, u32[]{:S(2)}) copy-start(bf16[768,256]{1,0:T(8,128)(2,1)} %targets.1) | copy-start | bytes 1179652
  2.3 3.2 %copy-start.5 = (s32[768]{0:T(1024)S(1)}, s32[768]{0:T(1024)}, u32[]{:S(2)}) copy-start(s32[768]{0:T(1024)} %param.10) | copy-start | bytes 9220
  2.3 3.2 %copy-start.6 = (s32[1,25]{1,0:T(1,128)S(1)}, s32[1,25]{1,0:T(1,128)}, u32[]{:S(2)}) copy-start(s32[1,25]{1,0:T(1,128)} %offsets.1) | copy-start | bytes 304
  2.4 4.0 %collective-permute-start = (bf16[784,256]{1,0:T(8,128)(2,1)S(1)}, bf16[784,256]{1,0:T(8,128)(2,1)S(1)}, u32[]{:S(2)}, u32[]{:S(2)}) collective-permute-start(bf16[784,256]{1,0:T(8,128)(2,1)S(1)} %shard_map.86.pack.refs_0_), channel_id=1, source_target_pairs={{0,1},{1,0},{2,3},{3,2},{4,5},{5,4},{6,7},{7,6},{8,9},{9,8},{10,11... | collective-permute-start | bytes 1204232 | tf_op jit(solution)/shard_map/ppermute | solution.py:252
  2.9 14.8 %collective-permute-start.1 = (bf16[784,256]{1,0:T(8,128)(2,1)S(1)}, bf16[784,256]{1,0:T(8,128)(2,1)S(1)}, u32[]{:S(2)}, u32[]{:S(2)}) collective-permute-start(bf16[784,256]{1,0:T(8,128)(2,1)S(1)} %shard_map.86.pack.refs_0_), channel_id=1, source_target_pairs={{0,2},{1,3},{2,0},{3,1},{4,6},{5,7},{6,4},{7,5},{8,10},{9,11},{10,... | collective-permute-start | bytes 1204232 | tf_op jit(solution)/shard_map/ppermute | solution.py:252
  5.5 2.2 %copy-start = (bf16[8192,256]{1,0:T(8,128)(2,1)S(1)}, bf16[8192,256]{1,0:T(8,128)(2,1)}, u32[]{:S(2)}) copy-start(bf16[8192,256]{1,0:T(8,128)(2,1)} %refs_4_.1) | copy-start | bytes 12582916
  5.5 2.2 %copy-start.3 = (s32[8192]{0:T(1024)S(1)}, s32[8192]{0:T(1024)}, u32[]{:S(2)}) copy-start(s32[8192]{0:T(1024)} %param.13) | copy-start | bytes 98308
  17.7 5.4 %collective-permute-start.2 = (bf16[784,256]{1,0:T(8,128)(2,1)S(1)}, bf16[784,256]{1,0:T(8,128)(2,1)S(1)}, u32[]{:S(2)}, u32[]{:S(2)}) collective-permute-start(bf16[784,256]{1,0:T(8,128)(2,1)S(1)} %collective-permute-done.1.refs_0_.refs_2_), channel_id=1, source_target_pairs={{0,1},{1,0},{2,3},{3,2},{4,5},{5,4},{6,7},{7,6},{8,9},{9,8},{10,11... | collective-permute-start | bytes 1204232 | tf_op jit(solution)/shard_map/ppermute | solution.py:252
  36.8 3.6 %collective-permute-start.3 = (f32[8,128]{1,0:T(8,128)S(1)}, f32[8,128]{1,0:T(8,128)S(1)}, u32[]{:S(2)}, u32[]{:S(2)}) collective-permute-start(f32[8,128]{1,0:T(8,128)S(1)} %get-tuple-element.13), channel_id=1, source_target_pairs={{0,4},{4,0},{8,12},{12,8},{16,20},{20,16},{24,28},{28,24},{1,5},{5... | collective-permute-start | bytes 12296 | tf_op jit(solution)/shard_map/ppermute | solution.py:252
  40.4 3.6 %collective-permute-start.4 = (f32[8,128]{1,0:T(8,128)S(1)}, f32[8,128]{1,0:T(8,128)S(1)}, u32[]{:S(2)}, u32[]{:S(2)}) collective-permute-start(f32[8,128]{1,0:T(8,128)S(1)} %add.9), channel_id=1, source_target_pairs={{0,8},{4,12},{8,0},{12,4},{16,24},{20,28},{24,16},{28,20},{1,9},{5... | collective-permute-start | bytes 12296 | tf_op jit(solution)/shard_map/ppermute | solution.py:252
  44.1 4.5 %collective-permute-start.5 = (f32[8,128]{1,0:T(8,128)S(1)}, f32[8,128]{1,0:T(8,128)S(1)}, u32[]{:S(2)}, u32[]{:S(2)}) collective-permute-start(f32[8,128]{1,0:T(8,128)S(1)} %add.10), channel_id=1, source_target_pairs={{0,16},{4,20},{8,24},{12,28},{16,0},{20,4},{24,8},{28,12},{1,17},{... | collective-permute-start | bytes 12296 | tf_op jit(solution)/shard_map/ppermute | solution.py:252

commit v2 on v1

--- a/solution.py
+++ b/solution.py
@@ -19,14 +19,28 @@
 LOWEST = 2.0**-90
 CONTRACT = (((1,), (1,)), ((), ()))
 VMEM = pl.BlockSpec(memory_space=pltpu.VMEM)
+HBM = pl.BlockSpec(memory_space=pltpu.HBM)
 SMEM = pl.BlockSpec(memory_space=pltpu.SMEM)
 
 
-def pack_kernel(users, places, out):
+def pack_kernel(me, users, places, targets, weights, negative_ids, offsets, *rest):
+    out, targets_here, live, id_rows, places_here, weights_here, offsets_here, done = rest
     tokens = users.shape[0]
     tiles = tokens // TILE
-    out[0:tokens, :] = users[...]
-    ids = places[...]
+    rows = tokens // LANES
+    pairs = [
+        (places, places_here),
+        (users, out.at[pl.ds(0, tokens), :]),
+        (weights, weights_here),
+        (offsets, offsets_here),
+        (negative_ids, id_rows),
+        (targets, targets_here),
+    ]
+    copies = [pltpu.make_async_copy(*pair, done.at[k]) for k, pair in enumerate(pairs)]
+    for copy in copies:
+        copy.start()
+    copies[0].wait()
+    ids = places_here[...]
     lines = []
     for digit in (ids & 127, (ids >> 7) & 127, ids >> 14):
         digit = digit.astype(jnp.float32)
@@ -38,6 +52,18 @@
             )
     lines.append(jnp.zeros((ID_ROWS - len(lines), TILE), jnp.float32))
     out[tokens:, :] = jnp.concatenate(lines, axis=0).astype(out.dtype)
+    copies[2].wait()
+    copies[3].wait()
+    line = lax.broadcasted_iota(jnp.int32, (rows, LANES), 0)
+    lane = lax.broadcasted_iota(jnp.int32, (rows, LANES), 1)
+    position = me[0] * tokens + line * LANES + lane
+    ends = offsets.shape[1]
+    has = position < offsets_here[0, ends - 1]
+    for user in range(1, ends):
+        has = has & (position + 1 != offsets_here[0, user])
+    live[...] = jnp.where(has, weights_here[...], 0).astype(jnp.float32)
+    for k in (1, 4, 5):
+        copies[k].wait()
 
 
 def tile_ids(pack, tile):
@@ -48,7 +74,7 @@
     return rows[0] + 128.0 * rows[1] + 16384.0 * rows[2]
 
 
-def sum_pack(scale2, pack, negs, id_rows, out, first):
+def sum_pack(scale2, pack, negs, id_rows, out, first, arrivals=None):
     tokens = pack.shape[0] - ID_ROWS
     number = negs.shape[0]
     tiles = tokens // TILE
@@ -58,6 +84,8 @@
     totals = [jnp.zeros((8, LANES), jnp.float32) for _ in range(2 * tiles)]
     for start in range(0, number, BLOCK):
         size = min(BLOCK, number - start)
+        if arrivals and start in arrivals:
+            arrivals[start].wait()
         block = negs[pl.ds(start, size), :]
         others = [
             jnp.broadcast_to(id_rows[row : row + 1, :], (LANES, LANES)).T
@@ -77,14 +105,27 @@
         out[first + row : first + row + 1, :] = jnp.sum(totals[row], axis=0, keepdims=True)
 
 
-def sums_kernel(scale2, count, *refs):
-    packs, (negs, id_rows, out) = refs[:count], refs[count:]
-    rows = (packs[0].shape[0] - ID_ROWS) // LANES
-    for k, pack in enumerate(packs):
-        sum_pack(scale2, pack, negs, id_rows, out, k * rows)
-
-
-def side_kernel(scale2, me, offsets, pack, targets, weights, out):
+def sums_kernel(scale2, pack, negs, id_rows, out):
+    sum_pack(scale2, pack, negs, id_rows, out, 0)
+
+
+def first_kernel(scale2, pack, other, targets, live, id_rows, far, *rest):
+    out, side, negs, arrived = rest
+    number = negs.shape[0]
+    rows = targets.shape[0] // LANES
+    edges = [0, min(2 * BLOCK, number), min(8 * BLOCK, number), number]
+    arrivals = {}
+    for k, (low, high) in enumerate(zip(edges, edges[1:])):
+        if low < high:
+            part = pl.ds(low, high - low)
+            arrivals[low] = pltpu.make_async_copy(far.at[part, :], negs.at[part, :], arrived.at[k])
+            arrivals[low].start()
+    side_rows(scale2, pack, targets, live, side)
+    sum_pack(scale2, pack, negs, id_rows, out, 0, arrivals)
+    sum_pack(scale2, other, negs, id_rows, out, rows)
+
+
+def side_rows(scale2, pack, targets, live, out):
     tokens = targets.shape[0]
     rows = tokens // LANES
     product = pack[0:tokens, :].astype(jnp.float32) * targets[...].astype(jnp.float32)
@@ -97,14 +138,7 @@
     positive = positive * scale2
     for row in range(rows):
         out[row : row + 1, :] = positive[0:1, row * LANES : (row + 1) * LANES]
-    line = lax.broadcasted_iota(jnp.int32, (rows, LANES), 0)
-    lane = lax.broadcasted_iota(jnp.int32, (rows, LANES), 1)
-    position = me[0] * tokens + line * LANES + lane
-    users = offsets.shape[1]
-    live = position < offsets[0, users - 1]
-    for user in range(1, users):
-        live = live & (position + 1 != offsets[0, user])
-    out[rows:, :] = jnp.where(live, weights[...], 0).astype(jnp.float32)
+    out[rows:, :] = live[...]
 
 
 def last_kernel(scale2, members, *refs):
@@ -236,14 +270,25 @@
     totals_out[...] = jnp.where(line == 0, first, jnp.where(line == 1, second, 0.0))
 
 
-def call(kernel, shapes, *args, flags=None, cost=None, scratch=(), smem=0, limit=16):
+def mean_kernel(totals, received, out):
+    totals = totals[...] + received[...]
+    weighted = jnp.sum(totals[0:1], axis=1, keepdims=True)
+    out[...] = weighted / jnp.sum(totals[1:2], axis=1, keepdims=True)
+
+
+def call(kernel, shapes, *args, cost=None, scratch=(), smem=0, far=(), limit=16):
+    specs = [SMEM] * smem + [VMEM] * (len(args) - smem)
+    args = list(args)
+    for place in far:
+        specs[place] = HBM
+        args[place] = pltpu.with_memory_space_constraint(args[place], pltpu.HBM)
     return pl.pallas_call(
         kernel,
         out_shape=shapes,
-        in_specs=[SMEM] * smem + [VMEM] * (len(args) - smem),
+        in_specs=specs,
         out_specs=jax.tree.map(lambda _: VMEM, shapes),
         scratch_shapes=list(scratch),
-        compiler_params=pltpu.CompilerParams(vmem_limit_bytes=limit * 2**20, flags=flags),
+        compiler_params=pltpu.CompilerParams(vmem_limit_bytes=limit * 2**20),
         cost_estimate=cost,
     )(*args)
 
@@ -278,39 +323,52 @@
             transcendentals=count * tokens * number,
         )
 
-    pack = call(
+    like = lambda array: jax.ShapeDtypeStruct(array.shape, array.dtype)
+    pack, targets, live, id_rows = call(
         pack_kernel,
-        jax.ShapeDtypeStruct((tokens + ID_ROWS, width), user_embed.dtype),
+        (
+            jax.ShapeDtypeStruct((tokens + ID_ROWS, width), user_embed.dtype),
+            like(positive_embed),
+            f32(rows, LANES),
+            like(id_rows),
+        ),
+        me,
         user_embed,
         positive_ids.reshape(rows, LANES),
-        cost=cost(1),
+        positive_embed,
+        token_weights.reshape(rows, LANES),
+        id_rows,
+        offsets,
+        smem=1,
+        far=range(1, 7),
+        scratch=[
+            pltpu.VMEM((rows, LANES), jnp.int32),
+            pltpu.VMEM((rows, LANES), jnp.int32),
+            pltpu.SMEM(offsets.shape, jnp.int32),
+            pltpu.SemaphoreType.DMA((6,)),
+        ],
+        limit=4,
     )
     packs = [pack, exchanged(pack, "neg", members, 1)]
     for mask in [2**k for k in range(1, members.bit_length() - 1)]:
         packs += [exchanged(pack, "neg", members, mask)] + [None] * (mask - 1)
-    side = call(
-        functools.partial(side_kernel, scale2),
-        f32(2 * rows, LANES),
-        me,
-        offsets,
-        pack,
-        positive_embed,
-        token_weights.reshape(rows, LANES),
-        smem=2,
-        cost=cost(1),
-    )
-    own, side = lax.optimization_barrier((pack, side))
-    early = [
-        call(
-            functools.partial(sums_kernel, scale2, 2),
+    shares, side, negatives = call(
+        functools.partial(first_kernel, scale2),
+        (
             f32(2 * rows, LANES),
-            own,
-            packs[1],
-            negative_embed,
-            id_rows,
-            cost=cost(2),
-        )
-    ]
+            f32(2 * rows, LANES),
+            like(negative_embed),
+        ),
+        *packs[:2],
+        targets,
+        live,
+        id_rows,
+        negative_embed,
+        far=(5,),
+        cost=cost(2),
+        scratch=[pltpu.SemaphoreType.DMA((3,))],
+    )
+    early = [shares]
     for mask in range(2, members):
         if packs[mask] is None:
             low = mask & -mask
@@ -319,10 +377,10 @@
     for mask in range(2, members - 1):
         early.append(
             call(
-                functools.partial(sums_kernel, scale2, 1),
+                functools.partial(sums_kernel, scale2),
                 f32(rows, LANES),
                 packs[mask],
-                negative_embed,
+                negatives,
                 id_rows,
                 cost=cost(1),
             )
@@ -332,7 +390,7 @@
         functools.partial(last_kernel, scale2, members),
         f32(lines + 2 * rows, LANES),
         *packs,
-        negative_embed,
+        negatives,
         id_rows,
         *early,
         side,
@@ -353,13 +411,16 @@
         me,
         gathered,
         smem=1,
+        limit=2,
     )
     mask = 1
     while mask < dp:
-        totals = totals + exchanged(totals, "dp", dp, mask)
+        received = exchanged(totals, "dp", dp, mask)
         mask *= 2
-    mean = jnp.sum(totals[0]) / jnp.sum(totals[1])
-    return (loss.reshape(tokens), mean)
+        if mask < dp:
+            totals = totals + received
+    mean = call(mean_kernel, f32(1, 1), totals, received, limit=1)
+    return (loss.reshape(tokens), mean.reshape(()))
 
 
 def solution(mesh):

time: 51.8 us -> 47.1 us (0.909)
  local copies, waits for them, and re-layouts: 2.96 us -> 0 us
  between operations: 3.15 us -> 0.69 us
  waiting for transfers between devices: 7.94 us -> 6.42 us
  starting transfers between devices: 7.12 us -> 8.62 us
  Pallas kernels: 24.6 us -> 25.9 us
  other arithmetic: 0.67 us -> 0.01 us
    unnamed x14 -> x0, local copies, waits for them, and re-layouts: 2.96 us -> none
    ppermute x6, waiting for transfers between devices: 7.94 us -> 6.42 us  [exchanged(): return lax.ppermute(value, axis, [(i, i ^ mask) for i in range(size)])]
    ppermute x6, starting transfers between devices: 7.12 us -> 8.62 us  [exchanged(): return lax.ppermute(value, axis, [(i, i ^ mask) for i in range(size)])]
    pallas_call x6, Pallas kernels: 24.6 us -> 25.9 us  [call(): pl.pallas_call(kernel, out_shape=shapes, in_specs=specs, out_specs=jax.tr...]
    reduce_sum x1 -> x0, other arithmetic: 0.66 us -> none  [shards(): mean = jnp.sum(totals[0]) / jnp.sum(totals[1])]
  transfers between devices with their start and end apart: 6 -> 6, of which waited for: 3 -> 3; matrix products, arithmetic and copies ran while one was open for 0% -> 0% of each run, Pallas kernels for 31% -> 34%
where the time goes in v2:
time: 47.1 us; the launch traced here: 47 us
  Pallas kernels  25.9 us (55%)
  starting transfers between devices  8.62 us (18%)
  waiting for transfers between devices  6.42 us (14%)
  blocking collectives  5.28 us (11%)
  between operations  0.69 us (1%)
    pallas_call x6, Pallas kernels, call(): pl.pallas_call(kernel, out_shape=shapes, in_specs=specs, out_specs=jax.tr...  25.9 us
    ppermute x6, starting transfers between devices, exchanged(): return lax.ppermute(value, axis, [(i, i ^ mask) for i in range(size)])  8.62 us
    ppermute x6, waiting for transfers between devices, exchanged(): return lax.ppermute(value, axis, [(i, i ^ mask) for i in range(size)])  6.42 us
    all_gather x1, blocking collectives, shards(): gathered = lax.all_gather(payload, 'neg', axis=0)  5.28 us
  transfers between devices with their start and end apart: 6, of which 3 were waited for; matrix products, arithmetic and copies ran while one was open for 0% of the time, Pallas kernels for 34%

profile of v2, /device:TPU:0, one launch (start us, length us, event | category | flops | bytes accessed | tf_op | source)
XLA Modules:
  0.0 47.0 jit_solution(13463154866874923139)
XLA Ops:
  0.6 1.2 %shard_map.86 = (bf16[784,256]{1,0:T(8,128)(2,1)S(1)}, bf16[768,256]{1,0:T(8,128)(2,1)S(1)}, f32[6,128]{1,0:T(8,128)S(1)}, s32[64,128]{1,0:T(8,128)S(1)}) custom-call(s32[1]{0:T(128)} %bitcast.me, bf16[768,256]{1,0:T(8,128)(2,1)} %users.1, s32[6,128]{1,0:T(8,128)} %bitcast.9, bf16[768,256]{1,0:T(8,128)(2,1)} %targets.1, s32[6,128]{1,0:T(8,128)} %bitcast.10, ...), custom_call_target="tpu_custom_call" | custom-call | tf_op jit(solution)/shard_map/pallas_call | solution.py:285
  1.9 0.6 %collective-permute-start = (bf16[784,256]{1,0:T(8,128)(2,1)S(1)}, bf16[784,256]{1,0:T(8,128)(2,1)S(1)}, u32[]{:S(2)}, u32[]{:S(2)}) collective-permute-start(bf16[784,256]{1,0:T(8,128)(2,1)S(1)} %get-tuple-element.13.pack.refs_0_), channel_id=1, source_target_pairs={{0,1},{1,0},{2,3},{3,2},{4,5},{5,4},{6,7},{7,6},{8,9},{9,8},{10,11... | collective-permute-start | bytes 1204232 | tf_op jit(solution)/shard_map/ppermute | solution.py:297
  2.4 2.6 %collective-permute-start.1 = (bf16[784,256]{1,0:T(8,128)(2,1)S(1)}, bf16[784,256]{1,0:T(8,128)(2,1)S(1)}, u32[]{:S(2)}, u32[]{:S(2)}) collective-permute-start(bf16[784,256]{1,0:T(8,128)(2,1)S(1)} %get-tuple-element.13.pack.refs_0_), channel_id=1, source_target_pairs={{0,2},{1,3},{2,0},{3,1},{4,6},{5,7},{6,4},{7,5},{8,10},{9,11},{10,... | collective-permute-start | bytes 1204232 | tf_op jit(solution)/shard_map/ppermute | solution.py:297
  5.0 0.0 collective-permute-done.other.refs_1_
  5.0 10.8 %shard_map.87 = (f32[12,128]{1,0:T(8,128)S(1)}, f32[12,128]{1,0:T(8,128)S(1)}, bf16[8192,256]{1,0:T(8,128)(2,1)S(1)}) custom-call(bf16[784,256]{1,0:T(8,128)(2,1)S(1)} %get-tuple-element.13.pack.refs_0_, bf16[784,256]{1,0:T(8,128)(2,1)S(1)} %collective-permute-done.other.refs_1_, bf16[768,256]{1,0:T(8,128)(2,1)S(1)} %get-tuple-element.14.targets, ...), custom_call_target="tpu_custom_call" | custom-call | flops 6442450944 | bytes 4194304 | tf_op jit(solution)/shard_map/pallas_call | solution.py:285
  15.8 0.0 collective-permute-done.1.pack.refs_2_
  15.8 0.2 collective-permute-start.2
  16.0 5.2 %shard_map.88.refs_7_ = f32[6,128]{1,0:T(8,128)S(1)} custom-call(bf16[784,256]{1,0:T(8,128)(2,1)S(1)} %collective-permute-done.1.pack.refs_2_, bf16[8192,256]{1,0:T(8,128)(2,1)S(1)} %get-tuple-element.19.negs.refs_4_, s32[64,128]{1,0:T(8,128)S(1)} %get-tuple-element.16.id_rows.refs_5_), custom_call_target="tpu_custom_call" | custom-call | flops 3221225472 | bytes 4194304 | tf_op jit(solution)/shard_map/pallas_call | solution.py:285
  21.2 0.0 collective-permute-done.2.refs_3_
  21.2 7.5 %shard_map.89 = f32[36,128]{1,0:T(8,128)S(1)} custom-call(bf16[784,256]{1,0:T(8,128)(2,1)S(1)} %get-tuple-element.13.pack.refs_0_, bf16[784,256]{1,0:T(8,128)(2,1)S(1)} %collective-permute-done.other.refs_1_, bf16[784,256]{1,0:T(8,128)(2,1)S(1)} %collective-permute-done.1.pack.refs_2_, bf16[784,256]{1,0:T(8,128)(2,1)S(1)} %collective-permute-done.2.refs_3_, ...), custom_call_target="tpu_custom_call" | custom-call | flops 3221225472 | bytes 4194304 | tf_op jit(solution)/shard_map/pallas_call | solution.py:285
  28.7 5.3 %all-gather.1.gathered = f32[4,36,128]{2,1,0:T(8,128)S(1)} all-gather(f32[1,36,128]{2,1,0:T(8,128)S(1)} %bitcast.7), channel_id=2, replica_groups=mesh['dp'=8,'neg'=4] {'neg'}, dimensions={0}, use_global_device_ids=true | all-gather | bytes 92160 | tf_op jit(solution)/shard_map/all_gather | solution.py:407
  34.0 0.6 %shard_map.90 = (f32[6,128]{1,0:T(8,128)}, f32[8,128]{1,0:T(8,128)S(1)}) custom-call(s32[1]{0:T(128)} %bitcast.me, f32[4,36,128]{2,1,0:T(8,128)S(1)} %all-gather.1.gathered), custom_call_target="tpu_custom_call" | custom-call | tf_op jit(solution)/shard_map/pallas_call | solution.py:285
  34.6 1.2 %collective-permute-start.3 = (f32[8,128]{1,0:T(8,128)S(1)}, f32[8,128]{1,0:T(8,128)S(1)}, u32[]{:S(2)}, u32[]{:S(2)}) collective-permute-start(f32[8,128]{1,0:T(8,128)S(1)} %get-tuple-element.23), channel_id=1, source_target_pairs={{0,4},{4,0},{8,12},{12,8},{16,20},{20,16},{24,28},{28,24},{1,5},{5... | collective-permute-start | bytes 12296 | tf_op jit(solution)/shard_map/ppermute | solution.py:297
  35.8 2.4 %collective-permute-done.3 = f32[8,128]{1,0:T(8,128)S(1)} collective-permute-done((f32[8,128]{1,0:T(8,128)S(1)}, f32[8,128]{1,0:T(8,128)S(1)}, u32[]{:S(2)}, u32[]{:S(2)}) %collective-permute-start.3) | collective-permute-done | bytes 4128 | tf_op jit(solution)/shard_map/ppermute | solution.py:297
  38.3 1.8 %collective-permute-start.4 = (f32[8,128]{1,0:T(8,128)S(1)}, f32[8,128]{1,0:T(8,128)S(1)}, u32[]{:S(2)}, u32[]{:S(2)}) collective-permute-start(f32[8,128]{1,0:T(8,128)S(1)} %add.6), channel_id=1, source_target_pairs={{0,8},{4,12},{8,0},{12,4},{16,24},{20,28},{24,16},{28,20},{1,9},{5... | collective-permute-start | bytes 12296 | tf_op jit(solution)/shard_map/ppermute | solution.py:297
  40.1 1.8 %collective-permute-done.4 = f32[8,128]{1,0:T(8,128)S(1)} collective-permute-done((f32[8,128]{1,0:T(8,128)S(1)}, f32[8,128]{1,0:T(8,128)S(1)}, u32[]{:S(2)}, u32[]{:S(2)}) %collective-permute-start.4) | collective-permute-done | bytes 4128 | tf_op jit(solution)/shard_map/ppermute | solution.py:297
  41.9 2.3 %collective-permute-start.5 = (f32[8,128]{1,0:T(8,128)S(1)}, f32[8,128]{1,0:T(8,128)S(1)}, u32[]{:S(2)}, u32[]{:S(2)}) collective-permute-start(f32[8,128]{1,0:T(8,128)S(1)} %add.7.totals), channel_id=1, source_target_pairs={{0,16},{4,20},{8,24},{12,28},{16,0},{20,4},{24,8},{28,12},{1,17},{... | collective-permute-start | bytes 12296 | tf_op jit(solution)/shard_map/ppermute | solution.py:297
  44.1 2.2 %collective-permute-done.5.received = f32[8,128]{1,0:T(8,128)S(1)} collective-permute-done((f32[8,128]{1,0:T(8,128)S(1)}, f32[8,128]{1,0:T(8,128)S(1)}, u32[]{:S(2)}, u32[]{:S(2)}) %collective-permute-start.5) | collective-permute-done | bytes 4128 | tf_op jit(solution)/shard_map/ppermute | solution.py:297
  46.4 0.6 %shard_map.91 = f32[1,1]{1,0:T(1,128)} custom-call(f32[8,128]{1,0:T(8,128)S(1)} %add.7.totals, f32[8,128]{1,0:T(8,128)S(1)} %collective-permute-done.5.received), custom_call_target="tpu_custom_call" | custom-call | tf_op jit(solution)/shard_map/pallas_call | solution.py:285
  (2 shorter events, 0.0 us)
Async XLA Ops:
  1.9 3.1 %collective-permute-start = (bf16[784,256]{1,0:T(8,128)(2,1)S(1)}, bf16[784,256]{1,0:T(8,128)(2,1)S(1)}, u32[]{:S(2)}, u32[]{:S(2)}) collective-permute-start(bf16[784,256]{1,0:T(8,128)(2,1)S(1)} %get-tuple-element.13.pack.refs_0_), channel_id=1, source_target_pairs={{0,1},{1,0},{2,3},{3,2},{4,5},{5,4},{6,7},{7,6},{8,9},{9,8},{10,11... | collective-permute-start | bytes 1204232 | tf_op jit(solution)/shard_map/ppermute | solution.py:297
  2.4 13.4 %collective-permute-start.1 = (bf16[784,256]{1,0:T(8,128)(2,1)S(1)}, bf16[784,256]{1,0:T(8,128)(2,1)S(1)}, u32[]{:S(2)}, u32[]{:S(2)}) collective-permute-start(bf16[784,256]{1,0:T(8,128)(2,1)S(1)} %get-tuple-element.13.pack.refs_0_), channel_id=1, source_target_pairs={{0,2},{1,3},{2,0},{3,1},{4,6},{5,7},{6,4},{7,5},{8,10},{9,11},{10,... | collective-permute-start | bytes 1204232 | tf_op jit(solution)/shard_map/ppermute | solution.py:297
  15.8 5.4 %collective-permute-start.2 = (bf16[784,256]{1,0:T(8,128)(2,1)S(1)}, bf16[784,256]{1,0:T(8,128)(2,1)S(1)}, u32[]{:S(2)}, u32[]{:S(2)}) collective-permute-start(bf16[784,256]{1,0:T(8,128)(2,1)S(1)} %collective-permute-done.1.pack.refs_2_), channel_id=1, source_target_pairs={{0,1},{1,0},{2,3},{3,2},{4,5},{5,4},{6,7},{7,6},{8,9},{9,8},{10,11... | collective-permute-start | bytes 1204232 | tf_op jit(solution)/shard_map/ppermute | solution.py:297
  34.6 3.6 %collective-permute-start.3 = (f32[8,128]{1,0:T(8,128)S(1)}, f32[8,128]{1,0:T(8,128)S(1)}, u32[]{:S(2)}, u32[]{:S(2)}) collective-permute-start(f32[8,128]{1,0:T(8,128)S(1)} %get-tuple-element.23), channel_id=1, source_target_pairs={{0,4},{4,0},{8,12},{12,8},{16,20},{20,16},{24,28},{28,24},{1,5},{5... | collective-permute-start | bytes 12296 | tf_op jit(solution)/shard_map/ppermute | solution.py:297
  38.3 3.6 %collective-permute-start.4 = (f32[8,128]{1,0:T(8,128)S(1)}, f32[8,128]{1,0:T(8,128)S(1)}, u32[]{:S(2)}, u32[]{:S(2)}) collective-permute-start(f32[8,128]{1,0:T(8,128)S(1)} %add.6), channel_id=1, source_target_pairs={{0,8},{4,12},{8,0},{12,4},{16,24},{20,28},{24,16},{28,20},{1,9},{5... | collective-permute-start | bytes 12296 | tf_op jit(solution)/shard_map/ppermute | solution.py:297
  41.9 4.5 %collective-permute-start.5 = (f32[8,128]{1,0:T(8,128)S(1)}, f32[8,128]{1,0:T(8,128)S(1)}, u32[]{:S(2)}, u32[]{:S(2)}) collective-permute-start(f32[8,128]{1,0:T(8,128)S(1)} %add.7.totals), channel_id=1, source_target_pairs={{0,16},{4,20},{8,24},{12,28},{16,0},{20,4},{24,8},{28,12},{1,17},{... | collective-permute-start | bytes 12296 | tf_op jit(solution)/shard_map/ppermute | solution.py:297

commit v3 on v2

--- a/solution.py
+++ b/solution.py
@@ -10,7 +10,7 @@
 
 LANES = 128
 TILE = 256
-BLOCK = 512
+BLOCK = 2048
 ID_ROWS = 16
 BATCH = 16
 LOG2E = math.log2(math.e)
@@ -21,8 +21,6 @@
 VMEM = pl.BlockSpec(memory_space=pltpu.VMEM)
 HBM = pl.BlockSpec(memory_space=pltpu.HBM)
 SMEM = pl.BlockSpec(memory_space=pltpu.SMEM)
-
-
 def pack_kernel(me, users, places, targets, weights, negative_ids, offsets, *rest):
     out, targets_here, live, id_rows, places_here, weights_here, offsets_here, done = rest
     tokens = users.shape[0]
@@ -82,14 +80,15 @@
         jnp.broadcast_to(tile_ids(pack, tile), (8, TILE)).astype(jnp.int32) for tile in range(tiles)
     ]
     totals = [jnp.zeros((8, LANES), jnp.float32) for _ in range(2 * tiles)]
-    for start in range(0, number, BLOCK):
-        size = min(BLOCK, number - start)
+    cuts = sorted({*range(0, number, BLOCK), *(arrivals or ()), number})
+    for start, stop in zip(cuts, cuts[1:]):
+        size = stop - start
         if arrivals and start in arrivals:
             arrivals[start].wait()
         block = negs[pl.ds(start, size), :]
         others = [
             jnp.broadcast_to(id_rows[row : row + 1, :], (LANES, LANES)).T
-            for row in range(start // LANES, (start + size) // LANES)
+            for row in range(start // LANES, stop // LANES)
         ]
         others = jnp.concatenate(others, axis=0).reshape(size // 8, 8, LANES)
         for tile in range(tiles):
@@ -113,7 +112,7 @@
     out, side, negs, arrived = rest
     number = negs.shape[0]
     rows = targets.shape[0] // LANES
-    edges = [0, min(2 * BLOCK, number), min(8 * BLOCK, number), number]
+    edges = [0, min(BLOCK // 4, number), min(BLOCK, number), number]
     arrivals = {}
     for k, (low, high) in enumerate(zip(edges, edges[1:])):
         if low < high:
@@ -144,7 +143,7 @@
 def last_kernel(scale2, members, *refs):
     packs = refs[:members]
     negs, id_rows, *rest = refs[members:]
-    early, side, out, sums, chosen, picked, mine, logits, values = (
+    early, side, out, sums, chosen, picked, mine, logits, values, wanted_ref = (
         rest[: members - 2],
         *rest[members - 2 :],
     )
@@ -163,7 +162,9 @@
     out[lines:, :] = side[...]
     bad = jnp.where(good, 0.0, 1.0)
 
-    @pl.when(jnp.max(bad) > 0.0)
+    count = jnp.sum(bad).astype(jnp.int32)
+
+    @pl.when(count > 0)
     def _():
         place = lax.broadcasted_iota(jnp.int32, (lines, LANES), 0) * LANES
         place = (place + lax.broadcasted_iota(jnp.int32, (lines, LANES), 1)).astype(jnp.float32)
@@ -174,10 +175,9 @@
             for tile in range(tokens // TILE):
                 row = tile_ids(pack, tile)
                 wanted += [row[:, :LANES], row[:, LANES:]]
-        wanted = jnp.concatenate(wanted, axis=0)
+        wanted_ref[...] = jnp.concatenate(wanted, axis=0)
         picked[...] = jnp.zeros_like(picked)
         mine[...] = jnp.zeros_like(mine)
-        count = jnp.sum(bad).astype(jnp.int32)
 
         def rescue(b, _):
             here = jnp.minimum(count - b * BATCH, BATCH)
@@ -188,8 +188,11 @@
                 at = found.astype(jnp.int32)
                 chosen[i] = at
                 sums[...] = jnp.where(left == found, beyond, left)
-                number_of = jnp.sum(jnp.where(place == found, wanted, 0.0))
-                mine[pl.ds(i, 1), :] = jnp.full((1, LANES), number_of, jnp.float32)
+                near = wanted_ref[pl.ds(at // LANES, 1), :]
+                lane = lax.broadcasted_iota(jnp.int32, (1, LANES), 1)
+                near = jnp.where(lane == lax.rem(at, LANES), near, 0.0)
+                near = jnp.sum(near, axis=1, keepdims=True)
+                mine[pl.ds(i, 1), :] = jnp.broadcast_to(near, (1, LANES))
                 inside = lax.rem(at, tokens)
                 line = lax.rem(inside, 16)
                 start = pl.multiple_of(inside - line, 16)
@@ -383,7 +386,7 @@
                 negatives,
                 id_rows,
                 cost=cost(1),
-            )
+                    )
         )
     lines = members * rows
     payload = call(
@@ -402,6 +405,7 @@
             pltpu.VMEM((BATCH, LANES), jnp.float32),
             pltpu.VMEM((number // LANES, BATCH, LANES), jnp.float32),
             pltpu.VMEM((BATCH, LANES), jnp.float32),
+            pltpu.VMEM((lines, LANES), jnp.float32),
         ],
     )
     gathered = lax.all_gather(payload, "neg", axis=0)

time: 47.1 us -> 46.3 us (0.983)
  Pallas kernels: 25.9 us -> 24.5 us
  starting transfers between devices: 8.62 us -> 10 us
  waiting for transfers between devices: 6.42 us -> 5.58 us
    pallas_call x6, Pallas kernels: 25.9 us -> 24.5 us  [call(): pl.pallas_call(kernel, out_shape=shapes, in_specs=specs, out_specs=jax.tr...]
    ppermute x6, starting transfers between devices: 8.62 us -> 10 us  [exchanged(): return lax.ppermute(value, axis, [(i, i ^ mask) for i in range(size)])]
    ppermute x6, waiting for transfers between devices: 6.42 us -> 5.58 us  [exchanged(): return lax.ppermute(value, axis, [(i, i ^ mask) for i in range(size)])]
  transfers between devices with their start and end apart: 6 -> 6, of which waited for: 3 -> 3; matrix products, arithmetic and copies ran while one was open for 0% -> 0% of each run, Pallas kernels for 34% -> 33%
where the time goes in v3:
time: 46.3 us; the launch traced here: 46.1 us
  Pallas kernels  24.5 us (53%)
  starting transfers between devices  10 us (22%)
  waiting for transfers between devices  5.58 us (12%)
  blocking collectives  5.28 us (11%)
  between operations  0.69 us (1%)
    pallas_call x6, Pallas kernels, call(): pl.pallas_call(kernel, out_shape=shapes, in_specs=specs, out_specs=jax.tr...  24.5 us
    ppermute x6, starting transfers between devices, exchanged(): return lax.ppermute(value, axis, [(i, i ^ mask) for i in range(size)])  10 us
    ppermute x6, waiting for transfers between devices, exchanged(): return lax.ppermute(value, axis, [(i, i ^ mask) for i in range(size)])  5.58 us
    all_gather x1, blocking collectives, shards(): gathered = lax.all_gather(payload, 'neg', axis=0)  5.28 us
  transfers between devices with their start and end apart: 6, of which 3 were waited for; matrix products, arithmetic and copies ran while one was open for 0% of the time, Pallas kernels for 33%

profile of v3, /device:TPU:0, one launch (start us, length us, event | category | flops | bytes accessed | tf_op | source)
XLA Modules:
  0.0 46.1 jit_solution(14717276394340889547)
XLA Ops:
  0.6 1.2 %shard_map.86 = (bf16[784,256]{1,0:T(8,128)(2,1)S(1)}, bf16[768,256]{1,0:T(8,128)(2,1)S(1)}, f32[6,128]{1,0:T(8,128)S(1)}, s32[64,128]{1,0:T(8,128)S(1)}) custom-call(s32[1]{0:T(128)} %bitcast.me, bf16[768,256]{1,0:T(8,128)(2,1)} %users.1, s32[6,128]{1,0:T(8,128)} %bitcast.9, bf16[768,256]{1,0:T(8,128)(2,1)} %targets.1, s32[6,128]{1,0:T(8,128)} %bitcast.10, ...), custom_call_target="tpu_custom_call" | custom-call | tf_op jit(solution)/shard_map/pallas_call | solution.py:288
  1.9 0.6 %collective-permute-start = (bf16[784,256]{1,0:T(8,128)(2,1)S(1)}, bf16[784,256]{1,0:T(8,128)(2,1)S(1)}, u32[]{:S(2)}, u32[]{:S(2)}) collective-permute-start(bf16[784,256]{1,0:T(8,128)(2,1)S(1)} %get-tuple-element.13.pack.refs_0_), channel_id=1, source_target_pairs={{0,1},{1,0},{2,3},{3,2},{4,5},{5,4},{6,7},{7,6},{8,9},{9,8},{10,11... | collective-permute-start | bytes 1204232 | tf_op jit(solution)/shard_map/ppermute | solution.py:300
  2.4 2.6 %collective-permute-start.1 = (bf16[784,256]{1,0:T(8,128)(2,1)S(1)}, bf16[784,256]{1,0:T(8,128)(2,1)S(1)}, u32[]{:S(2)}, u32[]{:S(2)}) collective-permute-start(bf16[784,256]{1,0:T(8,128)(2,1)S(1)} %get-tuple-element.13.pack.refs_0_), channel_id=1, source_target_pairs={{0,2},{1,3},{2,0},{3,1},{4,6},{5,7},{6,4},{7,5},{8,10},{9,11},{10,... | collective-permute-start | bytes 1204232 | tf_op jit(solution)/shard_map/ppermute | solution.py:300
  5.0 0.0 collective-permute-done.other.refs_1_
  5.0 10.6 %shard_map.87 = (f32[12,128]{1,0:T(8,128)S(1)}, f32[12,128]{1,0:T(8,128)S(1)}, bf16[8192,256]{1,0:T(8,128)(2,1)S(1)}) custom-call(bf16[784,256]{1,0:T(8,128)(2,1)S(1)} %get-tuple-element.13.pack.refs_0_, bf16[784,256]{1,0:T(8,128)(2,1)S(1)} %collective-permute-done.other.refs_1_, bf16[768,256]{1,0:T(8,128)(2,1)S(1)} %get-tuple-element.14.targets, ...), custom_call_target="tpu_custom_call" | custom-call | flops 6442450944 | bytes 4194304 | tf_op jit(solution)/shard_map/pallas_call | solution.py:288
  15.6 0.0 collective-permute-done.1.pack.refs_2_
  15.6 0.2 collective-permute-start.2
  15.9 4.8 %shard_map.88.refs_7_ = f32[6,128]{1,0:T(8,128)S(1)} custom-call(bf16[784,256]{1,0:T(8,128)(2,1)S(1)} %collective-permute-done.1.pack.refs_2_, bf16[8192,256]{1,0:T(8,128)(2,1)S(1)} %get-tuple-element.19.negs.refs_4_, s32[64,128]{1,0:T(8,128)S(1)} %get-tuple-element.16.id_rows.refs_5_), custom_call_target="tpu_custom_call" | custom-call | flops 3221225472 | bytes 4194304 | tf_op jit(solution)/shard_map/pallas_call | solution.py:288
  20.6 0.0 collective-permute-done.2.refs_3_
  20.7 6.6 %shard_map.89 = f32[36,128]{1,0:T(8,128)S(1)} custom-call(bf16[784,256]{1,0:T(8,128)(2,1)S(1)} %get-tuple-element.13.pack.refs_0_, bf16[784,256]{1,0:T(8,128)(2,1)S(1)} %collective-permute-done.other.refs_1_, bf16[784,256]{1,0:T(8,128)(2,1)S(1)} %collective-permute-done.1.pack.refs_2_, bf16[784,256]{1,0:T(8,128)(2,1)S(1)} %collective-permute-done.2.refs_3_, ...), custom_call_target="tpu_custom_call" | custom-call | flops 3221225472 | bytes 4194304 | tf_op jit(solution)/shard_map/pallas_call | solution.py:288
  27.3 5.3 %all-gather.1.gathered = f32[4,36,128]{2,1,0:T(8,128)S(1)} all-gather(f32[1,36,128]{2,1,0:T(8,128)S(1)} %bitcast.7), channel_id=2, replica_groups=mesh['dp'=8,'neg'=4] {'neg'}, dimensions={0}, use_global_device_ids=true | all-gather | bytes 92160 | tf_op jit(solution)/shard_map/all_gather | solution.py:411
  32.6 0.6 %shard_map.90 = (f32[6,128]{1,0:T(8,128)}, f32[8,128]{1,0:T(8,128)S(1)}) custom-call(s32[1]{0:T(128)} %bitcast.me, f32[4,36,128]{2,1,0:T(8,128)S(1)} %all-gather.1.gathered), custom_call_target="tpu_custom_call" | custom-call | tf_op jit(solution)/shard_map/pallas_call | solution.py:288
  33.2 2.6 %collective-permute-start.3 = (f32[8,128]{1,0:T(8,128)S(1)}, f32[8,128]{1,0:T(8,128)S(1)}, u32[]{:S(2)}, u32[]{:S(2)}) collective-permute-start(f32[8,128]{1,0:T(8,128)S(1)} %get-tuple-element.23), channel_id=1, source_target_pairs={{0,4},{4,0},{8,12},{12,8},{16,20},{20,16},{24,28},{28,24},{1,5},{5... | collective-permute-start | bytes 12296 | tf_op jit(solution)/shard_map/ppermute | solution.py:300
  35.8 1.6 %collective-permute-done.3 = f32[8,128]{1,0:T(8,128)S(1)} collective-permute-done((f32[8,128]{1,0:T(8,128)S(1)}, f32[8,128]{1,0:T(8,128)S(1)}, u32[]{:S(2)}, u32[]{:S(2)}) %collective-permute-start.3) | collective-permute-done | bytes 4128 | tf_op jit(solution)/shard_map/ppermute | solution.py:300
  37.4 1.8 %collective-permute-start.4 = (f32[8,128]{1,0:T(8,128)S(1)}, f32[8,128]{1,0:T(8,128)S(1)}, u32[]{:S(2)}, u32[]{:S(2)}) collective-permute-start(f32[8,128]{1,0:T(8,128)S(1)} %add.6), channel_id=1, source_target_pairs={{0,8},{4,12},{8,0},{12,4},{16,24},{20,28},{24,16},{28,20},{1,9},{5... | collective-permute-start | bytes 12296 | tf_op jit(solution)/shard_map/ppermute | solution.py:300
  39.1 1.8 %collective-permute-done.4 = f32[8,128]{1,0:T(8,128)S(1)} collective-permute-done((f32[8,128]{1,0:T(8,128)S(1)}, f32[8,128]{1,0:T(8,128)S(1)}, u32[]{:S(2)}, u32[]{:S(2)}) %collective-permute-start.4) | collective-permute-done | bytes 4128 | tf_op jit(solution)/shard_map/ppermute | solution.py:300
  41.0 2.4 %collective-permute-start.5 = (f32[8,128]{1,0:T(8,128)S(1)}, f32[8,128]{1,0:T(8,128)S(1)}, u32[]{:S(2)}, u32[]{:S(2)}) collective-permute-start(f32[8,128]{1,0:T(8,128)S(1)} %add.7.totals), channel_id=1, source_target_pairs={{0,16},{4,20},{8,24},{12,28},{16,0},{20,4},{24,8},{28,12},{1,17},{... | collective-permute-start | bytes 12296 | tf_op jit(solution)/shard_map/ppermute | solution.py:300
  43.3 2.2 %collective-permute-done.5.received = f32[8,128]{1,0:T(8,128)S(1)} collective-permute-done((f32[8,128]{1,0:T(8,128)S(1)}, f32[8,128]{1,0:T(8,128)S(1)}, u32[]{:S(2)}, u32[]{:S(2)}) %collective-permute-start.5) | collective-permute-done | bytes 4128 | tf_op jit(solution)/shard_map/ppermute | solution.py:300
  45.5 0.6 %shard_map.91 = f32[1,1]{1,0:T(1,128)} custom-call(f32[8,128]{1,0:T(8,128)S(1)} %add.7.totals, f32[8,128]{1,0:T(8,128)S(1)} %collective-permute-done.5.received), custom_call_target="tpu_custom_call" | custom-call | tf_op jit(solution)/shard_map/pallas_call | solution.py:288
  (2 shorter events, 0.0 us)
Async XLA Ops:
  1.9 3.1 %collective-permute-start = (bf16[784,256]{1,0:T(8,128)(2,1)S(1)}, bf16[784,256]{1,0:T(8,128)(2,1)S(1)}, u32[]{:S(2)}, u32[]{:S(2)}) collective-permute-start(bf16[784,256]{1,0:T(8,128)(2,1)S(1)} %get-tuple-element.13.pack.refs_0_), channel_id=1, source_target_pairs={{0,1},{1,0},{2,3},{3,2},{4,5},{5,4},{6,7},{7,6},{8,9},{9,8},{10,11... | collective-permute-start | bytes 1204232 | tf_op jit(solution)/shard_map/ppermute | solution.py:300
  2.4 13.2 %collective-permute-start.1 = (bf16[784,256]{1,0:T(8,128)(2,1)S(1)}, bf16[784,256]{1,0:T(8,128)(2,1)S(1)}, u32[]{:S(2)}, u32[]{:S(2)}) collective-permute-start(bf16[784,256]{1,0:T(8,128)(2,1)S(1)} %get-tuple-element.13.pack.refs_0_), channel_id=1, source_target_pairs={{0,2},{1,3},{2,0},{3,1},{4,6},{5,7},{6,4},{7,5},{8,10},{9,11},{10,... | collective-permute-start | bytes 1204232 | tf_op jit(solution)/shard_map/ppermute | solution.py:300
  15.6 5.0 %collective-permute-start.2 = (bf16[784,256]{1,0:T(8,128)(2,1)S(1)}, bf16[784,256]{1,0:T(8,128)(2,1)S(1)}, u32[]{:S(2)}, u32[]{:S(2)}) collective-permute-start(bf16[784,256]{1,0:T(8,128)(2,1)S(1)} %collective-permute-done.1.pack.refs_2_), channel_id=1, source_target_pairs={{0,1},{1,0},{2,3},{3,2},{4,5},{5,4},{6,7},{7,6},{8,9},{9,8},{10,11... | collective-permute-start | bytes 1204232 | tf_op jit(solution)/shard_map/ppermute | solution.py:300
  33.2 4.2 %collective-permute-start.3 = (f32[8,128]{1,0:T(8,128)S(1)}, f32[8,128]{1,0:T(8,128)S(1)}, u32[]{:S(2)}, u32[]{:S(2)}) collective-permute-start(f32[8,128]{1,0:T(8,128)S(1)} %get-tuple-element.23), channel_id=1, source_target_pairs={{0,4},{4,0},{8,12},{12,8},{16,20},{20,16},{24,28},{28,24},{1,5},{5... | collective-permute-start | bytes 12296 | tf_op jit(solution)/shard_map/ppermute | solution.py:300
  37.4 3.6 %collective-permute-start.4 = (f32[8,128]{1,0:T(8,128)S(1)}, f32[8,128]{1,0:T(8,128)S(1)}, u32[]{:S(2)}, u32[]{:S(2)}) collective-permute-start(f32[8,128]{1,0:T(8,128)S(1)} %add.6), channel_id=1, source_target_pairs={{0,8},{4,12},{8,0},{12,4},{16,24},{20,28},{24,16},{28,20},{1,9},{5... | collective-permute-start | bytes 12296 | tf_op jit(solution)/shard_map/ppermute | solution.py:300
  41.0 4.5 %collective-permute-start.5 = (f32[8,128]{1,0:T(8,128)S(1)}, f32[8,128]{1,0:T(8,128)S(1)}, u32[]{:S(2)}, u32[]{:S(2)}) collective-permute-start(f32[8,128]{1,0:T(8,128)S(1)} %add.7.totals), channel_id=1, source_target_pairs={{0,16},{4,20},{8,24},{12,28},{16,0},{20,4},{24,8},{28,12},{1,17},{... | collective-permute-start | bytes 12296 | tf_op jit(solution)/shard_map/ppermute | solution.py:300

commit v4 on v3

--- a/solution.py
+++ b/solution.py
@@ -7,6 +7,7 @@
 from jax.experimental import pallas as pl
 from jax.experimental.pallas import tpu as pltpu
 from jax.sharding import PartitionSpec as P
+
 
 LANES = 128
 TILE = 256
@@ -21,6 +22,8 @@
 VMEM = pl.BlockSpec(memory_space=pltpu.VMEM)
 HBM = pl.BlockSpec(memory_space=pltpu.HBM)
 SMEM = pl.BlockSpec(memory_space=pltpu.SMEM)
+
+
 def pack_kernel(me, users, places, targets, weights, negative_ids, offsets, *rest):
     out, targets_here, live, id_rows, places_here, weights_here, offsets_here, done = rest
     tokens = users.shape[0]
@@ -352,9 +355,9 @@
         ],
         limit=4,
     )
-    packs = [pack, exchanged(pack, "neg", members, 1)]
-    for mask in [2**k for k in range(1, members.bit_length() - 1)]:
-        packs += [exchanged(pack, "neg", members, mask)] + [None] * (mask - 1)
+    packs = [pack] + [None] * (members - 1)
+    for bit in reversed(range((members - 1).bit_length())):
+        packs[2**bit] = exchanged(pack, "neg", members, 2**bit)
     shares, side, negatives = call(
         functools.partial(first_kernel, scale2),
         (
@@ -380,13 +383,13 @@
     for mask in range(2, members - 1):
         early.append(
             call(
-                functools.partial(sums_kernel, scale2),
-                f32(rows, LANES),
-                packs[mask],
-                negatives,
-                id_rows,
-                cost=cost(1),
-                    )
+        functools.partial(sums_kernel, scale2),
+        f32(rows, LANES),
+        packs[mask],
+        negatives,
+        id_rows,
+        cost=cost(1),
+            )
         )
     lines = members * rows
     payload = call(

time: 46.3 us -> 45.9 us (level)
  transfers between devices with their start and end apart: 6 -> 6, of which waited for: 3 -> 3; matrix products, arithmetic and copies ran while one was open for 0% -> 0% of each run, Pallas kernels for 33% -> 34%
where the time goes in v4:
time: 45.9 us; the launch traced here: 45.7 us
  Pallas kernels  24.4 us (53%)
  starting transfers between devices  9.86 us (21%)
  blocking collectives  5.49 us (12%)
  waiting for transfers between devices  5.2 us (11%)
  between operations  0.69 us (2%)
    pallas_call x6, Pallas kernels, call(): pl.pallas_call(kernel, out_shape=shapes, in_specs=specs, out_specs=jax.tr...  24.4 us
    ppermute x6, starting transfers between devices, exchanged(): return lax.ppermute(value, axis, [(i, i ^ mask) for i in range(size)])  9.86 us
    all_gather x1, blocking collectives, shards(): gathered = lax.all_gather(payload, 'neg', axis=0)  5.49 us
    ppermute x6, waiting for transfers between devices, exchanged(): return lax.ppermute(value, axis, [(i, i ^ mask) for i in range(size)])  5.2 us
  transfers between devices with their start and end apart: 6, of which 3 were waited for; matrix products, arithmetic and copies ran while one was open for 0% of the time, Pallas kernels for 34%

profile of v4, /device:TPU:0, one launch (start us, length us, event | category | flops | bytes accessed | tf_op | source)
XLA Modules:
  0.0 45.7 jit_solution(14717276394340889547)
XLA Ops:
  0.6 1.2 %shard_map.86 = (bf16[784,256]{1,0:T(8,128)(2,1)S(1)}, bf16[768,256]{1,0:T(8,128)(2,1)S(1)}, f32[6,128]{1,0:T(8,128)S(1)}, s32[64,128]{1,0:T(8,128)S(1)}) custom-call(s32[1]{0:T(128)} %bitcast.me, bf16[768,256]{1,0:T(8,128)(2,1)} %users.1, s32[6,128]{1,0:T(8,128)} %bitcast.9, bf16[768,256]{1,0:T(8,128)(2,1)} %targets.1, s32[6,128]{1,0:T(8,128)} %bitcast.10, ...), custom_call_target="tpu_custom_call" | custom-call | tf_op jit(solution)/shard_map/pallas_call | solution.py:291
  1.9 0.6 %collective-permute-start = (bf16[784,256]{1,0:T(8,128)(2,1)S(1)}, bf16[784,256]{1,0:T(8,128)(2,1)S(1)}, u32[]{:S(2)}, u32[]{:S(2)}) collective-permute-start(bf16[784,256]{1,0:T(8,128)(2,1)S(1)} %get-tuple-element.13.pack.refs_0_), channel_id=1, source_target_pairs={{0,1},{1,0},{2,3},{3,2},{4,5},{5,4},{6,7},{7,6},{8,9},{9,8},{10,11... | collective-permute-start | bytes 1204232 | tf_op jit(solution)/shard_map/ppermute | solution.py:303
  2.4 2.6 %collective-permute-start.1 = (bf16[784,256]{1,0:T(8,128)(2,1)S(1)}, bf16[784,256]{1,0:T(8,128)(2,1)S(1)}, u32[]{:S(2)}, u32[]{:S(2)}) collective-permute-start(bf16[784,256]{1,0:T(8,128)(2,1)S(1)} %get-tuple-element.13.pack.refs_0_), channel_id=1, source_target_pairs={{0,2},{1,3},{2,0},{3,1},{4,6},{5,7},{6,4},{7,5},{8,10},{9,11},{10,... | collective-permute-start | bytes 1204232 | tf_op jit(solution)/shard_map/ppermute | solution.py:303
  5.0 0.0 collective-permute-done.other.refs_1_
  5.0 10.6 %shard_map.87 = (f32[12,128]{1,0:T(8,128)S(1)}, f32[12,128]{1,0:T(8,128)S(1)}, bf16[8192,256]{1,0:T(8,128)(2,1)S(1)}) custom-call(bf16[784,256]{1,0:T(8,128)(2,1)S(1)} %get-tuple-element.13.pack.refs_0_, bf16[784,256]{1,0:T(8,128)(2,1)S(1)} %collective-permute-done.other.refs_1_, bf16[768,256]{1,0:T(8,128)(2,1)S(1)} %get-tuple-element.14.targets, ...), custom_call_target="tpu_custom_call" | custom-call | flops 6442450944 | bytes 4194304 | tf_op jit(solution)/shard_map/pallas_call | solution.py:291
  15.6 0.0 collective-permute-done.1.pack.refs_2_
  15.6 0.2 collective-permute-start.2
  15.9 4.8 %shard_map.88.refs_7_ = f32[6,128]{1,0:T(8,128)S(1)} custom-call(bf16[784,256]{1,0:T(8,128)(2,1)S(1)} %collective-permute-done.1.pack.refs_2_, bf16[8192,256]{1,0:T(8,128)(2,1)S(1)} %get-tuple-element.19.negs.refs_4_, s32[64,128]{1,0:T(8,128)S(1)} %get-tuple-element.16.id_rows.refs_5_), custom_call_target="tpu_custom_call" | custom-call | flops 3221225472 | bytes 4194304 | tf_op jit(solution)/shard_map/pallas_call | solution.py:291
  20.6 0.0 collective-permute-done.2.refs_3_
  20.7 6.6 %shard_map.89 = f32[36,128]{1,0:T(8,128)S(1)} custom-call(bf16[784,256]{1,0:T(8,128)(2,1)S(1)} %get-tuple-element.13.pack.refs_0_, bf16[784,256]{1,0:T(8,128)(2,1)S(1)} %collective-permute-done.other.refs_1_, bf16[784,256]{1,0:T(8,128)(2,1)S(1)} %collective-permute-done.1.pack.refs_2_, bf16[784,256]{1,0:T(8,128)(2,1)S(1)} %collective-permute-done.2.refs_3_, ...), custom_call_target="tpu_custom_call" | custom-call | flops 3221225472 | bytes 4194304 | tf_op jit(solution)/shard_map/pallas_call | solution.py:291
  27.3 5.5 %all-gather.1.gathered = f32[4,36,128]{2,1,0:T(8,128)S(1)} all-gather(f32[1,36,128]{2,1,0:T(8,128)S(1)} %bitcast.7), channel_id=2, replica_groups=mesh['dp'=8,'neg'=4] {'neg'}, dimensions={0}, use_global_device_ids=true | all-gather | bytes 92160 | tf_op jit(solution)/shard_map/all_gather | solution.py:414
  32.7 0.6 %shard_map.90 = (f32[6,128]{1,0:T(8,128)}, f32[8,128]{1,0:T(8,128)S(1)}) custom-call(s32[1]{0:T(128)} %bitcast.me, f32[4,36,128]{2,1,0:T(8,128)S(1)} %all-gather.1.gathered), custom_call_target="tpu_custom_call" | custom-call | tf_op jit(solution)/shard_map/pallas_call | solution.py:291
  33.4 2.0 %collective-permute-start.3 = (f32[8,128]{1,0:T(8,128)S(1)}, f32[8,128]{1,0:T(8,128)S(1)}, u32[]{:S(2)}, u32[]{:S(2)}) collective-permute-start(f32[8,128]{1,0:T(8,128)S(1)} %get-tuple-element.23), channel_id=1, source_target_pairs={{0,4},{4,0},{8,12},{12,8},{16,20},{20,16},{24,28},{28,24},{1,5},{5... | collective-permute-start | bytes 12296 | tf_op jit(solution)/shard_map/ppermute | solution.py:303
  35.3 1.6 %collective-permute-done.3 = f32[8,128]{1,0:T(8,128)S(1)} collective-permute-done((f32[8,128]{1,0:T(8,128)S(1)}, f32[8,128]{1,0:T(8,128)S(1)}, u32[]{:S(2)}, u32[]{:S(2)}) %collective-permute-start.3) | collective-permute-done | bytes 4128 | tf_op jit(solution)/shard_map/ppermute | solution.py:303
  37.0 1.7 %collective-permute-start.4 = (f32[8,128]{1,0:T(8,128)S(1)}, f32[8,128]{1,0:T(8,128)S(1)}, u32[]{:S(2)}, u32[]{:S(2)}) collective-permute-start(f32[8,128]{1,0:T(8,128)S(1)} %add.6), channel_id=1, source_target_pairs={{0,8},{4,12},{8,0},{12,4},{16,24},{20,28},{24,16},{28,20},{1,9},{5... | collective-permute-start | bytes 12296 | tf_op jit(solution)/shard_map/ppermute | solution.py:303
  38.7 1.9 %collective-permute-done.4 = f32[8,128]{1,0:T(8,128)S(1)} collective-permute-done((f32[8,128]{1,0:T(8,128)S(1)}, f32[8,128]{1,0:T(8,128)S(1)}, u32[]{:S(2)}, u32[]{:S(2)}) %collective-permute-start.4) | collective-permute-done | bytes 4128 | tf_op jit(solution)/shard_map/ppermute | solution.py:303
  40.6 2.8 %collective-permute-start.5 = (f32[8,128]{1,0:T(8,128)S(1)}, f32[8,128]{1,0:T(8,128)S(1)}, u32[]{:S(2)}, u32[]{:S(2)}) collective-permute-start(f32[8,128]{1,0:T(8,128)S(1)} %add.7.totals), channel_id=1, source_target_pairs={{0,16},{4,20},{8,24},{12,28},{16,0},{20,4},{24,8},{28,12},{1,17},{... | collective-permute-start | bytes 12296 | tf_op jit(solution)/shard_map/ppermute | solution.py:303
  43.4 1.7 %collective-permute-done.5.received = f32[8,128]{1,0:T(8,128)S(1)} collective-permute-done((f32[8,128]{1,0:T(8,128)S(1)}, f32[8,128]{1,0:T(8,128)S(1)}, u32[]{:S(2)}, u32[]{:S(2)}) %collective-permute-start.5) | collective-permute-done | bytes 4128 | tf_op jit(solution)/shard_map/ppermute | solution.py:303
  45.1 0.6 %shard_map.91 = f32[1,1]{1,0:T(1,128)} custom-call(f32[8,128]{1,0:T(8,128)S(1)} %add.7.totals, f32[8,128]{1,0:T(8,128)S(1)} %collective-permute-done.5.received), custom_call_target="tpu_custom_call" | custom-call | tf_op jit(solution)/shard_map/pallas_call | solution.py:291
  (2 shorter events, 0.0 us)
Async XLA Ops:
  1.9 3.1 %collective-permute-start = (bf16[784,256]{1,0:T(8,128)(2,1)S(1)}, bf16[784,256]{1,0:T(8,128)(2,1)S(1)}, u32[]{:S(2)}, u32[]{:S(2)}) collective-permute-start(bf16[784,256]{1,0:T(8,128)(2,1)S(1)} %get-tuple-element.13.pack.refs_0_), channel_id=1, source_target_pairs={{0,1},{1,0},{2,3},{3,2},{4,5},{5,4},{6,7},{7,6},{8,9},{9,8},{10,11... | collective-permute-start | bytes 1204232 | tf_op jit(solution)/shard_map/ppermute | solution.py:303
  2.4 13.2 %collective-permute-start.1 = (bf16[784,256]{1,0:T(8,128)(2,1)S(1)}, bf16[784,256]{1,0:T(8,128)(2,1)S(1)}, u32[]{:S(2)}, u32[]{:S(2)}) collective-permute-start(bf16[784,256]{1,0:T(8,128)(2,1)S(1)} %get-tuple-element.13.pack.refs_0_), channel_id=1, source_target_pairs={{0,2},{1,3},{2,0},{3,1},{4,6},{5,7},{6,4},{7,5},{8,10},{9,11},{10,... | collective-permute-start | bytes 1204232 | tf_op jit(solution)/shard_map/ppermute | solution.py:303
  15.6 5.0 %collective-permute-start.2 = (bf16[784,256]{1,0:T(8,128)(2,1)S(1)}, bf16[784,256]{1,0:T(8,128)(2,1)S(1)}, u32[]{:S(2)}, u32[]{:S(2)}) collective-permute-start(bf16[784,256]{1,0:T(8,128)(2,1)S(1)} %collective-permute-done.1.pack.refs_2_), channel_id=1, source_target_pairs={{0,1},{1,0},{2,3},{3,2},{4,5},{5,4},{6,7},{7,6},{8,9},{9,8},{10,11... | collective-permute-start | bytes 1204232 | tf_op jit(solution)/shard_map/ppermute | solution.py:303
  33.4 3.6 %collective-permute-start.3 = (f32[8,128]{1,0:T(8,128)S(1)}, f32[8,128]{1,0:T(8,128)S(1)}, u32[]{:S(2)}, u32[]{:S(2)}) collective-permute-start(f32[8,128]{1,0:T(8,128)S(1)} %get-tuple-element.23), channel_id=1, source_target_pairs={{0,4},{4,0},{8,12},{12,8},{16,20},{20,16},{24,28},{28,24},{1,5},{5... | collective-permute-start | bytes 12296 | tf_op jit(solution)/shard_map/ppermute | solution.py:303
  37.0 3.6 %collective-permute-start.4 = (f32[8,128]{1,0:T(8,128)S(1)}, f32[8,128]{1,0:T(8,128)S(1)}, u32[]{:S(2)}, u32[]{:S(2)}) collective-permute-start(f32[8,128]{1,0:T(8,128)S(1)} %add.6), channel_id=1, source_target_pairs={{0,8},{4,12},{8,0},{12,4},{16,24},{20,28},{24,16},{28,20},{1,9},{5... | collective-permute-start | bytes 12296 | tf_op jit(solution)/shard_map/ppermute | solution.py:303
  40.6 4.5 %collective-permute-start.5 = (f32[8,128]{1,0:T(8,128)S(1)}, f32[8,128]{1,0:T(8,128)S(1)}, u32[]{:S(2)}, u32[]{:S(2)}) collective-permute-start(f32[8,128]{1,0:T(8,128)S(1)} %add.7.totals), channel_id=1, source_target_pairs={{0,16},{4,20},{8,24},{12,28},{16,0},{20,4},{24,8},{28,12},{1,17},{... | collective-permute-start | bytes 12296 | tf_op jit(solution)/shard_map/ppermute | solution.py:303
